TPU v7x, 32 devices: a whole 2x2x4 slice. The times are simulated.
32 devices in a mesh: ka: 8 (over z, y), ga: 4 (over x, core).
Axes of the slice: x: 2, y: 2, z: 4, core: 2. Of those that a mesh axis runs over, the one named last changes fastest.
Arguments:
- x_dens: bfloat16 [32, 64, 1500], P('ka', None, 'ga'), may hold values from -6 to 6
- y_dens: bfloat16 [32, 64, 1500], P('ka', None, 'ga'), may hold values from -0.15625 to 0.15625
- p_dens: bfloat16 [32, 64, 1500], P('ka', None, 'ga'), may hold values from -1 to 1
- coulomb: float32 [1500], P('ga'), may hold values from 0.1 to 2
- screened: bfloat16 [16, 1500, 1500], P('ka', 'ga'), may hold values from -0.15625 to 0.15625
- pairs: int32 [128, 3], P('ka'), may hold values from 0 to 31, as said below
- q_slot: int32 [16], replicated, may hold values from 0 to 15, as said below
Outputs:
- blocks: float32 [128, 4096], P('ka')
- mirrored: float32 [32, 4096], P('ka')
Inputs may be any that keep to these rules, and one draw needn't show every extreme that they name: `pairs`: column 0 of the rows held by index d of ka lies in d * 4 to (d + 1) * 4 - 1; column 1 is any k-point; column 2 is a momentum transfer below 16. Among one index's 16 rows at most 2 have a second k-point held by one same index, and this is reached; at most 2 have q_slot[q] // 2 equal to one same value, and this is reached. `q_slot`: A permutation of the slots; slot s of screened is held by index s // 2 of ka.
All inputs are finite; a program needn't handle non-finite values.
Results may differ from a plain program's by a relative error of at most 0.0014.
Values may be sent and summed in bfloat16 or wider, within the bound.
A program may use at most 192 MiB of HBM per device.

v0:
```python
import functools
import jax
import jax.numpy as jnp
from jax import lax
from jax.experimental import pallas as pl
from jax.experimental.pallas import tpu as pltpu
from jax.sharding import PartitionSpec as P

CAPQ = 2
F32 = jnp.float32
BF16 = jnp.bfloat16
VM = pl.BlockSpec(memory_space=pltpu.VMEM)
SM = pl.BlockSpec(memory_space=pltpu.SMEM)
LIMIT = 66000000


class Gather:
    def __init__(self, n, src, out, send, recv):
        self.n, self.nz = n, n // 2
        self.me = lax.axis_index("ka")
        self.z, self.y = self.me // 2, self.me % 2
        self.src, self.out, self.send, self.recv = src, out, send, recv
        self.size = src.shape[0]
        self.cut = self.size - max(1, self.size // 6)

    def copy(self, zz, yy, half, way, own=False):
        first, length = (self.cut, self.size - self.cut) if half else (0, self.cut)
        block = self.out.at[pl.ds((zz * 2 + yy) * self.size + first, length)]
        source = self.src.at[pl.ds(first, length)] if own else block
        index = (zz * 2 + yy) * 2 + half
        if way == 2:
            target = self.z * 2 + 1 - self.y
        else:
            step = 1 if way == 0 else -1
            target = (self.z + step) * 2 + self.y
        return pltpu.make_async_remote_copy(
            src_ref=source,
            dst_ref=block,
            send_sem=self.send.at[way * 2 * self.n + index],
            recv_sem=self.recv.at[index],
            device_id={"ka": target},
            device_id_type=pl.DeviceIdType.MESH,
        )

    def chain(self, zz, yy, half, act, ways=(0, 1), own=False):
        for way in ways:
            free = self.z < self.nz - 1 if way == 0 else self.z > 0

            @pl.when(free)
            def _(way=way):
                act(self.copy(zz, yy, half, way, own))

    def first(self):
        start = lambda c: c.start()
        self.copy(self.z, self.y, 1, 2, True).start()
        self.chain(self.z, self.y, 0, start, own=True)
        self.chain(self.z, self.y, 1, start, own=True)
        self.copy(self.z, self.y, 0, 2, True).start()
        self.out[pl.ds(self.me * self.size, self.size)] = self.src[...]

    def second(self):
        start = lambda c: c.start()
        self.copy(self.z, 1 - self.y, 1, 2).wait_recv()
        self.chain(self.z, 1 - self.y, 1, start)

    def hop(self, h):
        start = lambda c: c.start()
        for way in (0, 1):
            zz = self.z - h if way == 0 else self.z + h
            there = zz >= 0 if way == 0 else zz < self.nz

            @pl.when(there)
            def _(zz=zz, way=way):
                for yy, half in ((self.y, 0), (self.y, 1), (1 - self.y, 1)):
                    self.copy(zz, yy, half, 2).wait_recv()
                    self.chain(zz, yy, half, start, (way,))
                    if half == 0:
                        self.copy(zz, yy, 0, 2).start()

    def finish(self):
        done = lambda c: c.wait_send()
        self.copy(self.z, self.y, 1, 2, True).wait_send()
        for half in (0, 1):
            self.chain(self.z, self.y, half, done, own=True)
        self.copy(self.z, self.y, 0, 2, True).wait_send()
        self.chain(self.z, 1 - self.y, 1, done)
        self.copy(self.z, 1 - self.y, 0, 2).wait_recv()

        def tail(h, carry):
            for way in (0, 1):
                zz = self.z - h if way == 0 else self.z + h
                there = zz >= 0 if way == 0 else zz < self.nz

                @pl.when(there)
                def _(zz=zz, way=way):
                    for yy, half in ((self.y, 0), (self.y, 1), (1 - self.y, 1)):
                        self.chain(zz, yy, half, done, (way,))
                    self.copy(zz, self.y, 0, 2).wait_send()
                    self.copy(zz, 1 - self.y, 0, 2).wait_recv()

            return carry

        lax.fori_loop(1, self.nz, tail, 0)


def run_gathers(gathers):
    for g in gathers:
        g.first()
    for g in gathers:
        g.second()

    def body(h, carry):
        for g in gathers:
            g.hop(h)
        return carry

    lax.fori_loop(1, gathers[0].nz, body, 0)
    for g in gathers:
        g.finish()


def greet(n, ka_too, ga_too, all_ka=False):
    barrier = pltpu.get_barrier_semaphore()
    me = lax.axis_index("ka")
    z, y = me // 2, me % 2
    nz = n // 2
    targets = []
    if ka_too:
        targets += [{"ka": lax.rem(z + 1, nz) * 2 + y}, {"ka": lax.rem(z + nz - 1, nz) * 2 + y}]
        targets += [{"ka": z * 2 + 1 - y}]
    if all_ka:
        targets += [{"ka": lax.rem(me + i, n)} for i in range(1, n)]
    if ga_too:
        g = lax.axis_index("ga")
        n_ga = lax.axis_size("ga")
        targets += [{"ga": lax.rem(g + i, n_ga)} for i in range(1, n_ga)]
    for t in targets:
        pl.semaphore_signal(barrier, inc=1, device_id=t, device_id_type=pl.DeviceIdType.MESH)
    pl.semaphore_wait(barrier, len(targets))


def gather_sems(n):
    return [pltpu.SemaphoreType.DMA((6 * n,)), pltpu.SemaphoreType.DMA((2 * n,))]


def params(collective_id):
    return pltpu.CompilerParams(
        collective_id=collective_id, has_side_effects=True, vmem_limit_bytes=LIMIT
    )


def first_kernel(n, x_ref, l_ref, xo_ref, lo_ref, xs, xr, ls, lr):
    greet(n, True, False)
    run_gathers([Gather(n, l_ref, lo_ref, ls, lr), Gather(n, x_ref, xo_ref, xs, xr)])


def table_kernel(n, rows, q_slots, list_ref, qs_ref, k_ref, k2_ref, at_ref, w_at, count):
    me = lax.axis_index("ka")
    slots = n * CAPQ

    def clear(s, c):
        k_ref[s] = 0
        k2_ref[s] = -1
        w_at[s] = 0
        return c

    lax.fori_loop(0, slots, clear, 0)

    def source(a, c):
        def zero(o, c):
            count[o] = 0
            return c

        lax.fori_loop(0, n, zero, 0)

        def pair(j, c):
            r = a * rows + j
            slot = qs_ref[list_ref[r * 3 + 2]]
            owner = slot // q_slots
            rank = count[owner]
            count[owner] = rank + 1
            at_ref[r] = owner * CAPQ + rank

            @pl.when(owner == me)
            def _():
                s = a * CAPQ + rank
                k_ref[s] = list_ref[r * 3]
                k2_ref[s] = list_ref[r * 3 + 1]
                w_at[s] = slot % q_slots

            return c

        return lax.fori_loop(0, rows, pair, c)

    lax.fori_loop(0, n, source, 0)


def reduce_two(part, out, recv1, tsend, recv2, s1, r1, s2, r2, pieces):
    g = lax.axis_index("ga")
    x, c = g // 2, g % 2
    per = part.shape[1] // pieces
    there, here = 1 - x, x

    def one(t, xx, i):
        rows = pl.ds(i * per, per)
        return pltpu.make_async_remote_copy(
            src_ref=part.at[xx * 2 + 1 - c, rows],
            dst_ref=recv1.at[xx, rows],
            send_sem=s1.at[t * pieces + i],
            recv_sem=r1.at[t * pieces + i],
            device_id={"ga": x * 2 + 1 - c},
            device_id_type=pl.DeviceIdType.MESH,
        )

    def two(i):
        rows = pl.ds(i * per, per)
        return pltpu.make_async_remote_copy(
            src_ref=tsend.at[rows],
            dst_ref=recv2.at[rows],
            send_sem=s2.at[i],
            recv_sem=r2.at[i],
            device_id={"ga": there * 2 + c},
            device_id_type=pl.DeviceIdType.MESH,
        )

    def begin(i):
        one(0, there, i).start()
        one(1, here, i).start()

    def middle():
        for i in range(pieces):
            rows = pl.ds(i * per, per)
            one(0, there, i).wait_recv()
            v = part[there * 2 + c, rows].astype(F32) + recv1[there, rows].astype(F32)
            tsend[rows] = v.astype(tsend.dtype)
            two(i).start()

    def end():
        for i in range(pieces):
            rows = pl.ds(i * per, per)
            one(1, here, i).wait_recv()
            two(i).wait_recv()
            v = part[here * 2 + c, rows].astype(F32) + recv1[here, rows].astype(F32)
            out[rows] = (v + recv2[rows].astype(F32)).astype(out.dtype)
        for i in range(pieces):
            one(0, there, i).wait_send()
            one(1, here, i).wait_send()
            two(i).wait_send()

    return begin, middle, end


def second_kernel(n, pieces, k_ref, w_at, x_ref, w_ref, y_ref, p_ref, half_ref, yo_ref, po_ref, part,
                  recv1, tsend, recv2, s1, r1, s2, r2, ys, yr, ps, pr):
    greet(n, True, True)
    gathers = [Gather(n, y_ref, yo_ref, ys, yr), Gather(n, p_ref, po_ref, ps, pr)]
    for g in gathers:
        g.first()
    begin, middle, end = reduce_two(part, half_ref, recv1, tsend, recv2, s1, r1, s2, r2, pieces)
    n_ga, width = part.shape[0], part.shape[3]
    per = part.shape[1] // pieces

    def multiply(s, c):
        v = jnp.dot(x_ref[k_ref[s]], w_ref[w_at[s]], preferred_element_type=F32)
        for i in range(n_ga):
            part[i, s] = v[:, i * width : (i + 1) * width].astype(part.dtype)
        return c

    for i in range(pieces):
        if i == pieces // 2:
            for g in gathers:
                g.second()
        lax.fori_loop(i * per, (i + 1) * per, multiply, 0)
        begin(i)
    middle()

    def body(h, carry):
        for g in gathers:
            g.hop(h)
        return carry

    lax.fori_loop(1, gathers[0].nz, body, 0)
    for g in gathers:
        g.finish()
    end()


def block_kernel(n, k_ref, k2_ref, half_ref, y_ref, p_ref, v_ref, o_ref):
    n_ga, quarter = o_ref.shape[0], o_ref.shape[2]
    dims = (((1,), (1,)), ((), ()))

    def source(a, carry):
        both = []
        for c in range(CAPQ):
            s = a * CAPQ + c
            k, k2 = k_ref[s], jnp.maximum(k2_ref[s], 0)
            direct = lax.dot_general(half_ref[s], y_ref[k2], dims, preferred_element_type=F32)
            weighted = p_ref[k].astype(F32) * v_ref[...]
            high = weighted.astype(BF16)
            low = (weighted - high.astype(F32)).astype(BF16)
            other = p_ref[k2]
            term = lax.dot_general(high, other, dims, preferred_element_type=F32)
            term += lax.dot_general(low, other, dims, preferred_element_type=F32)
            both.append(2.0 * term - direct)
        v = jnp.concatenate(both, axis=1)
        for i in range(n_ga):
            o_ref[i, a] = v[i * quarter : (i + 1) * quarter]
        return carry

    lax.fori_loop(0, n, source, 0)


def tail_kernel(n, rows, per_dev, k2_ref, at_ref, part, out, own, recv1, tsend, recv2, second,
                outbox, inbox, lines, s1, r1, s2, r2, as_, ar, gs, gr):
    greet(n, False, True, True)
    begin, middle, end = reduce_two(part, own, recv1, tsend, recv2, s1, r1, s2, r2, 1)
    begin(0)
    me = lax.axis_index("ka")
    g = lax.axis_index("ga")
    n_ga = out.shape[0]
    shape = own.shape[1:]
    nt = shape[1] // CAPQ
    left = lax.broadcasted_iota(jnp.int32, shape, 1) < nt
    for a in range(n):
        second[a] = jnp.where(left, k2_ref[a * CAPQ], k2_ref[a * CAPQ + 1])
    middle()
    end()
    pairs = per_dev // 2

    def summed(k):
        total = jnp.zeros(shape, F32)
        for a in range(n):
            total += jnp.where(second[a] == k, own[a], 0.0)
        return total[:, :nt] + total[:, nt:]

    def fill(b, carry):
        outbox[b, 0] = own[b]
        for i in range(pairs):
            k = b * per_dev + i
            outbox[b, 1 + i] = jnp.concatenate([summed(k), summed(k + pairs)], axis=1)
        return carry

    lax.fori_loop(0, n, fill, 0)

    def cross(i):
        to = lax.rem(me + i, n)
        return pltpu.make_async_remote_copy(
            src_ref=outbox.at[to],
            dst_ref=inbox.at[me],
            send_sem=as_.at[i],
            recv_sem=ar.at[i],
            device_id={"ka": to},
            device_id_type=pl.DeviceIdType.MESH,
        )

    for i in range(1, n):
        cross(i).start()
    inbox[me] = outbox[me]
    for i in range(1, n):
        cross(i).wait()

    def tile(j):
        at = at_ref[me * rows + j]
        both = inbox[at // CAPQ, 0]
        return jnp.where(at % CAPQ == 0, both[:, :nt], both[:, nt:])

    for j in range(rows // 2):
        lines[j] = jnp.concatenate([tile(j), tile(j + rows // 2)], axis=1)
    for i in range(pairs):
        total = inbox[0, 1 + i]
        for o in range(1, n):
            total += inbox[o, 1 + i]
        lines[rows // 2 + i] = total
    copies = [
        pltpu.make_async_remote_copy(
            src_ref=lines,
            dst_ref=out.at[g],
            send_sem=gs.at[i],
            recv_sem=gr.at[i],
            device_id={"ga": lax.rem(g + i, n_ga)},
            device_id_type=pl.DeviceIdType.MESH,
        )
        for i in range(1, n_ga)
    ]
    for c in copies:
        c.start()
    out[g] = lines[...]
    for c in copies:
        c.wait()


def per_device(x_dens, y_dens, p_dens, coulomb, screened, pairs, q_slot):
    n = lax.axis_size("ka")
    n_ga = lax.axis_size("ga")
    per_dev, nt, g = x_dens.shape
    q_slots = screened.shape[0]
    rows = pairs.shape[0]
    slots = n * CAPQ
    shape = jax.ShapeDtypeStruct
    listed = jnp.pad(pairs, ((0, 0), (0, 128 - pairs.shape[1]))).reshape(2, rows // 2, 128)
    x_all, listed = pl.pallas_call(
        functools.partial(first_kernel, n),
        out_shape=[shape((n * per_dev, nt, g), BF16), shape((n * 2, rows // 2, 128), jnp.int32)],
        in_specs=[VM, VM],
        out_specs=[VM, VM],
        scratch_shapes=gather_sems(n) + gather_sems(n),
        compiler_params=params(0),
        name="gather_x",
    )(x_dens, listed)
    listed = listed.reshape(n * rows, 128)[:, :3].reshape(n * rows * 3)
    wide = F32 if slots * nt <= 2048 else BF16
    ints = lambda m: shape((m,), jnp.int32)
    k_at, k2_at, at, w_at = pl.pallas_call(
        functools.partial(table_kernel, n, rows, q_slots),
        out_shape=[ints(slots), ints(slots), ints(n * rows), ints(slots)],
        in_specs=[SM, SM],
        out_specs=[SM] * 4,
        scratch_shapes=[pltpu.SMEM((n,), jnp.int32)],
        name="tables",
    )(listed, q_slot)
    pieces = 4
    half, y_all, p_all = pl.pallas_call(
        functools.partial(second_kernel, n, pieces),
        out_shape=[shape((slots, nt, g), BF16)] + [shape((n * per_dev, nt, g), BF16)] * 2,
        in_specs=[SM, SM, VM, VM, VM, VM],
        out_specs=[VM, VM, VM],
        scratch_shapes=[
            pltpu.VMEM((n_ga, slots, nt, g), wide),
            pltpu.VMEM((2, slots, nt, g), wide),
            pltpu.VMEM((slots, nt, g), BF16),
            pltpu.VMEM((slots, nt, g), BF16),
            pltpu.SemaphoreType.DMA((2 * pieces,)),
            pltpu.SemaphoreType.DMA((2 * pieces,)),
            pltpu.SemaphoreType.DMA((pieces,)),
            pltpu.SemaphoreType.DMA((pieces,)),
        ]
        + gather_sems(n)
        + gather_sems(n),
        compiler_params=params(1),
        name="reduce_gather",
    )(k_at, w_at, x_all, screened, y_dens, p_dens)
    quarter = nt // n_ga
    block = pl.pallas_call(
        functools.partial(block_kernel, n),
        out_shape=shape((n_ga, n, quarter, CAPQ * nt), F32),
        in_specs=[SM, SM, VM, VM, VM, VM],
        out_specs=VM,
        compiler_params=pltpu.CompilerParams(vmem_limit_bytes=LIMIT),
        name="block",
    )(k_at, k2_at, half, y_all, p_all, coulomb.reshape(1, g))
    line = (n, quarter, CAPQ * nt)
    lines = rows // 2 + per_dev // 2
    each = line[1:]
    full = pl.pallas_call(
        functools.partial(tail_kernel, n, rows, per_dev),
        out_shape=shape((n_ga, lines) + each, F32),
        in_specs=[SM, SM, VM],
        out_specs=VM,
        scratch_shapes=[
            pltpu.VMEM(line, F32),
            pltpu.VMEM((2,) + line, F32),
            pltpu.VMEM(line, F32),
            pltpu.VMEM(line, F32),
            pltpu.VMEM(line, jnp.int32),
            pltpu.VMEM((n, 1 + per_dev // 2) + each, F32),
            pltpu.VMEM((n, 1 + per_dev // 2) + each, F32),
            pltpu.VMEM((lines,) + each, F32),
        ]
        + [pltpu.SemaphoreType.DMA((2,))] * 4
        + [pltpu.SemaphoreType.DMA((n,))] * 2
        + [pltpu.SemaphoreType.DMA((n_ga,))] * 2,
        compiler_params=params(2),
        name="tail",
    )(k2_at, at, block)
    split = lambda v: jnp.concatenate([v[..., :nt], v[..., nt:]], axis=1)
    blocks = split(full[:, : rows // 2]).transpose(1, 0, 2, 3).reshape(rows, nt * nt)
    mirrored = split(full[:, rows // 2 :]).transpose(1, 3, 0, 2).reshape(per_dev, nt * nt)
    return (blocks, mirrored)


def solution(mesh):
    in_specs = (
        P("ka", None, "ga"),
        P("ka", None, "ga"),
        P("ka", None, "ga"),
        P("ga"),
        P("ka", "ga", None),
        P("ka", None),
        P(),
    )
    out_specs = (P("ka", None), P("ka", None))
    return jax.shard_map(
        per_device, mesh=mesh, in_specs=in_specs, out_specs=out_specs, check_vma=False
    )
```

profile of v0, /device:TPU:0, one launch (start us, length us, event | category | flops | bytes accessed | tf_op | source)
XLA Modules:
  0.0 114.3 jit_solution(13497227622506883544)
XLA Ops:
  0.6 0.8 copy.15
  1.4 0.6 pad_bitcast_fusion.l_ref
  2.0 30.6 %gather_x.1 = (bf16[32,64,375]{2,1,0:T(8,128)(2,1)}, s32[16,8,128]{2,1,0:T(8,128)}) custom-call(bf16[4,64,375]{2,1,0:T(8,128)(2,1)} %x_ref.1, s32[2,8,128]{2,1,0:T(8,128)} %pad_bitcast_fusion.l_ref), custom_call_target="tpu_custom_call" | custom-call | tf_op jit(solution)/shard_map/gather_x/pallas_call | solution.py:401
  32.6 1.6 %reshape.24.list_ref = s32[384]{0:T(512)} reshape(s32[128,3]{1,0:T(8,128)} %bitcast.10) | data formatting | bytes 3072 | tf_op jit(solution)/shard_map/reshape | solution.py:410
  34.2 5.0 %tables.1 = (s32[16]{0:T(128)}, s32[16]{0:T(128)}, s32[128]{0:T(128)}, s32[16]{0:T(128)}) custom-call(s32[384]{0:T(512)} %reshape.24.list_ref, s32[16]{0:T(128)} %qs_ref.1), custom_call_target="tpu_custom_call" | custom-call | tf_op jit(solution)/shard_map/tables/pallas_call | solution.py:413
  39.2 3.3 %copy.12.w_ref = bf16[2,375,1500]{2,1,0:T(8,128)(2,1)} copy(bf16[2,375,1500]{2,0,1:T(2,128)(2,1)} %param.11) | data formatting | bytes 4500000 | tf_op args[4]
  42.5 0.0 copy-start
  42.5 43.7 %reduce_gather.1 = (bf16[16,64,375]{2,1,0:T(8,128)(2,1)}, bf16[32,64,375]{2,1,0:T(8,128)(2,1)}, bf16[32,64,375]{2,1,0:T(8,128)(2,1)}) custom-call(s32[16]{0:T(128)} %get-tuple-element.14.k_ref, s32[16]{0:T(128)} %get-tuple-element.15.w_at, bf16[32,64,375]{2,1,0:T(8,128)(2,1)} %get-tuple-element.16.x_ref, bf16[2,375,1500]{2,1,0:T(8,128)(2,1)} %copy.12.w_ref, ...), custom_call_target="tpu_custom_call" | custom-call | tf_op jit(solution)/shard_map/reduce_gather/pallas_call | solution.py:422
  86.2 0.0 copy-done
  86.2 0.6 reshape.25.v_ref
  86.8 5.4 %block.1.part = f32[4,8,16,128]{3,2,1,0:T(8,128)} custom-call(s32[16]{0:T(128)} %get-tuple-element.14.k_ref, s32[16]{0:T(128)} %get-tuple-element.12.k2_ref, bf16[16,64,375]{2,1,0:T(8,128)(2,1)} %get-tuple-element.17.half_ref, bf16[32,64,375]{2,1,0:T(8,128)(2,1)} %get-tuple-element.18.y_ref, bf16[32,64,375]{2,1,0:T(8,128)(2,1)} %get-tuple-element.19.p_ref, ...), custom_call_target="tpu_custom_call" | custom-call | tf_op jit(solution)/shard_map/block/pallas_call | solution.py:443
  92.2 17.6 %tail.1 = f32[4,10,16,128]{3,2,1,0:T(8,128)} custom-call(s32[16]{0:T(128)} %get-tuple-element.12.k2_ref, s32[128]{0:T(128)} %get-tuple-element.13.at_ref, f32[4,8,16,128]{3,2,1,0:T(8,128)} %block.1.part), custom_call_target="tpu_custom_call" | custom-call | tf_op jit(solution)/shard_map/tail/pallas_call | solution.py:454
  109.9 1.2 %fusion.1 = (f32[4,8,16,64]{3,2,1,0:T(8,128)S(1)}, f32[4,8,16,64]{3,2,1,0:T(8,128)S(1)}) fusion(f32[4,10,16,128]{3,2,1,0:T(8,128)} %tail.1), kind=kLoop, calls=%fused_computation.4 | loop fusion | bytes 524288 | tf_op jit(solution)/shard_map/slice | solution.py:475
  111.1 0.9 reshape.26
  112.0 1.0 fusion
  113.0 0.2 copy.14
  113.3 1.1 reshape.27
  (3 shorter events, 0.1 us)
Async XLA Ops:
  42.5 43.7 %copy-start = (f32[375]{0:T(512)S(1)}, f32[375]{0:T(512)}, u32[]{:S(2)}) copy-start(f32[375]{0:T(512)} %param.10) | copy-start | bytes 4504
where the time goes:
time: 116 us; the launch traced here: 114 us
  Pallas kernels  102 us (88%)
  local copies, waits for them, and re-layouts  11.2 us (10%)
    pallas_call x1, Pallas kernels, per_device(): pl.pallas_call(functools.partial(second_kernel, n, pieces), out_shape=[sh...  43.7 us
    pallas_call x1, Pallas kernels, per_device(): pl.pallas_call(functools.partial(first_kernel, n), out_shape=[shape((n *...  30.6 us
    pallas_call x1, Pallas kernels, per_device(): pl.pallas_call(functools.partial(tail_kernel, n, rows, per_dev), out_shap...  17.6 us
    pallas_call x1, Pallas kernels, per_device(): pl.pallas_call(functools.partial(block_kernel, n), out_shape=shape((n_ga,...  5.42 us
    pallas_call x1, Pallas kernels, per_device(): pl.pallas_call(functools.partial(table_kernel, n, rows, q_slots), out_sha...  5 us
    unnamed x4, local copies, waits for them, and re-layouts  4.04 us

commit v1 on v0

v1 whole, which is shorter than its diff:
```python
import functools
import jax
import jax.numpy as jnp
from jax import lax
from jax.experimental import pallas as pl
from jax.experimental.pallas import tpu as pltpu
from jax.sharding import PartitionSpec as P

CAPQ = 2
F32 = jnp.float32
BF16 = jnp.bfloat16
I32 = jnp.int32
VM = pl.BlockSpec(memory_space=pltpu.VMEM)
SM = pl.BlockSpec(memory_space=pltpu.SMEM)
HB = pl.BlockSpec(memory_space=pl.ANY)
LIMIT = 66000000
DIMS = (((1,), (1,)), ((), ()))


def start(c):
    c.start()


def sent(c):
    c.wait_send()


def remote(src, dst, ss, rs, to):
    return pltpu.make_async_remote_copy(
        src_ref=src,
        dst_ref=dst,
        send_sem=ss,
        recv_sem=rs,
        device_id=to,
        device_id_type=pl.DeviceIdType.MESH,
    )


def greet(n):
    barrier = pltpu.get_barrier_semaphore()
    me = lax.axis_index("ka")
    g = lax.axis_index("ga")
    n_ga = lax.axis_size("ga")

    def hello(to):
        pl.semaphore_signal(barrier, inc=1, device_id=to, device_id_type=pl.DeviceIdType.MESH)

    lax.fori_loop(1, n, lambda i, c: (hello({"ka": lax.rem(me + i, n)}), c)[1], 0)
    for i in range(1, n_ga):
        hello({"ga": lax.rem(g + i, n_ga)})
    pl.semaphore_wait(barrier, n - 1 + n_ga - 1)


class Gather:
    def __init__(self, n, src, out, send, recv, cut):
        self.n, self.nz = n, n // 2
        self.me = lax.axis_index("ka")
        self.z, self.y = self.me // 2, self.me % 2
        self.src, self.out, self.send, self.recv = src, out, send, recv
        self.size = src.shape[0]
        self.cut = cut

    def copy(self, zz, yy, k, way, own=False):
        at = (zz * 2 + yy) * self.size + k
        block = self.out.at[at]
        if way == 2:
            target = self.z * 2 + 1 - self.y
        else:
            target = (self.z + (1 if way == 0 else -1)) * 2 + self.y
        return remote(
            self.src.at[k] if own else block,
            block,
            self.send.at[way * self.n * self.size + at],
            self.recv.at[at],
            {"ka": target},
        )

    def chain(self, zz, yy, k, act, ways=(0, 1), own=False):
        for way in ways:
            free = self.z < self.nz - 1 if way == 0 else self.z > 0

            @pl.when(free)
            def _(way=way):
                act(self.copy(zz, yy, k, way, own))

    def early(self):
        return range(self.cut, self.size)

    def first(self):
        for k in self.early():
            self.copy(self.z, self.y, k, 2, True).start()
        for k in range(self.size):
            self.chain(self.z, self.y, k, start, own=True)
        for k in range(self.cut):
            self.copy(self.z, self.y, k, 2, True).start()
        self.out[pl.ds(self.me * self.size, self.size)] = self.src[...]

    def second(self):
        for k in self.early():
            self.copy(self.z, 1 - self.y, k, 2).wait_recv()
            self.chain(self.z, 1 - self.y, k, start)

    def sides(self, h, act):
        for way in (0, 1):
            zz = self.z - h if way == 0 else self.z + h
            there = zz >= 0 if way == 0 else zz < self.nz

            @pl.when(there)
            def _(zz=zz, way=way):
                act(zz, way)

    def hop(self, h):
        def one(k, yy, zz, way):
            self.copy(zz, yy, k, 2).wait_recv()
            self.chain(zz, yy, k, start, (way,))

        for k in range(self.size):

            def own(zz, way, k=k):
                one(k, self.y, zz, way)
                if k < self.cut:
                    self.copy(zz, self.y, k, 2).start()

            self.sides(h, own)
        for k in self.early():
            self.sides(h, lambda zz, way, k=k: one(k, 1 - self.y, zz, way))

    def finish(self):
        for k in range(self.size):
            self.chain(self.z, self.y, k, sent, own=True)
            self.copy(self.z, self.y, k, 2, True).wait_send()
        for k in self.early():
            self.chain(self.z, 1 - self.y, k, sent)
        for k in range(self.cut):
            self.copy(self.z, 1 - self.y, k, 2).wait_recv()

        def tail(h, carry):
            def side(zz, way):
                for k in range(self.size):
                    self.chain(zz, self.y, k, sent, (way,))
                for k in self.early():
                    self.chain(zz, 1 - self.y, k, sent, (way,))
                for k in range(self.cut):
                    self.copy(zz, self.y, k, 2).wait_send()
                    self.copy(zz, 1 - self.y, k, 2).wait_recv()

            self.sides(h, side)
            return carry

        lax.fori_loop(1, self.nz, tail, 0)


class Pick:
    def __init__(self, n, src, col, out, got, tab, send, recv, ps, pr):
        self.n, self.nz = n, n // 2
        self.me = lax.axis_index("ka")
        self.z, self.y = self.me // 2, self.me % 2
        self.src, self.col, self.out, self.got, self.tab = src, col, out, got, tab
        self.send, self.recv, self.ps, self.pr = send, recv, ps, pr
        self.size = src.shape[0]

    def copy(self, zz, k, way, own=False):
        at = zz * self.size + k
        target = (self.z + (1 if way == 0 else -1)) * 2 + self.y
        return remote(
            self.src.at[k] if own else self.col.at[at],
            self.col.at[at],
            self.send.at[way * self.nz * self.size + at],
            self.recv.at[at],
            {"ka": target},
        )

    def chain(self, zz, k, act, ways=(0, 1), own=False):
        for way in ways:
            free = self.z < self.nz - 1 if way == 0 else self.z > 0

            @pl.when(free)
            def _(way=way):
                act(self.copy(zz, k, way, own))

    def sides(self, h, act):
        for way in (0, 1):
            zz = self.z - h if way == 0 else self.z + h
            there = zz >= 0 if way == 0 else zz < self.nz

            @pl.when(there)
            def _(zz=zz, way=way):
                act(zz, way)

    def first(self):
        for k in range(self.size):
            self.chain(self.z, k, start, own=True)
        self.col[pl.ds(self.z * self.size, self.size)] = self.src[...]

    def hop(self, h):
        for k in range(self.size):

            def one(zz, way, k=k):
                self.copy(zz, k, way).wait_recv()
                self.chain(zz, k, start, (way,))

            self.sides(h, one)

    def chosen(self, zz, owner, r):
        which = self.tab[zz * 2 + self.y, owner * CAPQ + r]
        v = self.col[zz * self.size]
        for k in range(1, self.size):
            v = jnp.where(which == k, self.col[zz * self.size + k], v)
        return v

    def across(self, zz):
        rows = pl.ds(zz * CAPQ, CAPQ)
        return remote(
            self.out.at[rows],
            self.got.at[rows],
            self.ps.at[zz],
            self.pr.at[zz],
            {"ka": self.z * 2 + 1 - self.y},
        )

    def pass_on(self, zz):
        for r in range(CAPQ):
            self.out[zz * CAPQ + r] = self.chosen(zz, self.z * 2 + 1 - self.y, r)
        self.across(zz).start()

    def finish(self):
        for k in range(self.size):
            self.chain(self.z, k, sent, own=True)
        self.across(self.z).wait_send()

        def tail(h, carry):
            def side(zz, way):
                for k in range(self.size):
                    self.chain(zz, k, sent, (way,))
                self.across(zz).wait_send()

            self.sides(h, side)
            return carry

        lax.fori_loop(1, self.nz, tail, 0)


class Reduce:
    def __init__(self, part, out, recv1, tsend, recv2, s1, r1, s2, r2, per):
        self.g = lax.axis_index("ga")
        self.x, self.c = self.g // 2, self.g % 2
        self.part, self.out = part, out
        self.recv1, self.tsend, self.recv2 = recv1, tsend, recv2
        self.s1, self.r1, self.s2, self.r2, self.per = s1, r1, s2, r2, per

    def rows(self, i):
        return pl.ds(i * self.per, self.per)

    def one(self, t, i):
        xx = self.x if t else 1 - self.x
        return remote(
            self.part.at[xx * 2 + 1 - self.c, self.rows(i)],
            self.recv1.at[xx, self.rows(i)],
            self.s1.at[i * 2 + t],
            self.r1.at[i * 2 + t],
            {"ga": self.x * 2 + 1 - self.c},
        )

    def two(self, i):
        return remote(
            self.tsend.at[self.rows(i)],
            self.recv2.at[self.rows(i)],
            self.s2.at[i],
            self.r2.at[i],
            {"ga": (1 - self.x) * 2 + self.c},
        )

    def sum_one(self, xx, i):
        v = self.part[xx * 2 + self.c, self.rows(i)].astype(F32)
        return v + self.recv1[xx, self.rows(i)].astype(F32)

    def begin(self, i):
        self.one(0, i).start()
        self.one(1, i).start()

    def middle(self, i):
        self.one(0, i).wait_recv()
        self.tsend[self.rows(i)] = self.sum_one(1 - self.x, i).astype(self.tsend.dtype)
        self.two(i).start()

    def end(self, i):
        self.one(1, i).wait_recv()
        v = self.sum_one(self.x, i)
        self.two(i).wait_recv()
        v = v + self.recv2[self.rows(i)].astype(F32)
        self.out[self.rows(i)] = v.astype(self.out.dtype)
        self.one(0, i).wait_send()
        self.one(1, i).wait_send()
        self.two(i).wait_send()


def make_row(n, q_slots, per_dev, pairs_ref, qs_ref, tab, at_ref, kept):
    me = lax.axis_index("ka")
    rows = pairs_ref.shape[1]
    slots = n * CAPQ
    owners = []
    for j in range(rows):
        slot = qs_ref[pairs_ref[2, j]]
        owner = slot // q_slots
        rank = jnp.int32(0)
        for o in owners:
            rank = rank + jnp.where(o == owner, 1, 0)
        owners.append(owner)
        at_ref[j] = owner * CAPQ + rank
        kept[0, j] = pairs_ref[0, j] - me * per_dev
        kept[1, j] = slot - owner * q_slots
        kept[2, j] = pairs_ref[1, j]

    def one(s, carry):
        found = [jnp.int32(0), jnp.int32(0), jnp.int32(-1)]
        for j in range(rows):
            hit = at_ref[j] == s
            for i in range(3):
                found[i] = jnp.where(hit, kept[i, j], found[i])
        for i in range(3):
            tab[me, i * slots + s] = found[i]
        return carry

    lax.fori_loop(0, slots, one, 0)


def kernel(n, pairs_ref, qs_ref, x_ref, y_ref, p_ref, v_ref, w_hbm, blocks_ref, mirr_ref,
           tab, at_ref, kept, wt, w_ref, x_col, x_out, x_got, y_all, p_all, part, half,
           recv1, tsend, recv2, part2, own, q1, qt, q2, second, outbox, inbox, lines, turned, flat,
           ws, ts, tr, xs, xr, xps, xpr, ys, yr, ps, pr, s1, r1, s2, r2, t1, u1, t2, u2,
           as_, ar, gs, gr):
    per_dev, nt, width = x_ref.shape
    rows = pairs_ref.shape[1]
    q_slots = w_ref.shape[0]
    nz = n // 2
    slots = n * CAPQ
    n_ga = part.shape[0]
    me = lax.axis_index("ka")
    g = lax.axis_index("ga")
    z, y = me // 2, me % 2
    fetch = pltpu.make_async_copy(w_hbm, wt, ws)
    fetch.start()
    greet(n)
    xg = Pick(n, x_ref, x_col, x_out, x_got, tab, xs, xr, xps, xpr)
    yg = Gather(n, y_ref, y_all, ys, yr, per_dev - 1)
    pg = Gather(n, p_ref, p_all, ps, pr, per_dev - 1)
    xg.first()
    make_row(n, q_slots, per_dev, pairs_ref, qs_ref, tab, at_ref, kept)

    def row(i, whose):
        return remote(
            tab.at[whose], tab.at[whose], ts.at[i], tr.at[whose], {"ka": lax.rem(me + i, n)}
        )

    lax.fori_loop(1, n, lambda i, c: (row(i, me).start(), c)[1], 0)
    xg.pass_on(z)
    fetch.wait()
    for s in range(q_slots):
        w_ref[s] = wt[:, s, :]
    red = Reduce(part, half, recv1, tsend, recv2, s1, r1, s2, r2, 2 * CAPQ)

    def multiply(v, a, r):
        w = tab[a, slots + me * CAPQ + r]
        v = jnp.dot(v, w_ref[w], preferred_element_type=F32)
        for i in range(n_ga):
            part[i, a * CAPQ + r] = v[:, i * width : (i + 1) * width].astype(part.dtype)

    def piece(zz):
        for r in range(CAPQ):
            multiply(xg.chosen(zz, me, r), zz * 2 + y, r)
        xg.across(zz).wait_recv()
        for r in range(CAPQ):
            multiply(x_got[zz * CAPQ + r], zz * 2 + 1 - y, r)
        red.begin(zz)

    xg.hop(1)
    yg.first()
    lax.fori_loop(
        1, n, lambda i, c: (row(i, lax.rem(me + n - i, n)).wait_recv(), c)[1], 0
    )
    xg.sides(1, lambda zz, way: xg.pass_on(zz))
    piece(z)
    yg.second()

    def stage(h, carry):
        xg.hop(h)
        xg.sides(h, lambda zz, way: xg.pass_on(zz))

        @pl.when(h == 2)
        def _():
            pg.first()
            red.middle(z)

        xg.sides(h - 1, lambda zz, way: piece(zz))

        @pl.when(h > 2)
        def _():
            xg.sides(h - 2, lambda zz, way: red.middle(zz))

        return carry

    lax.fori_loop(2, nz, stage, 0)
    pg.second()
    xg.sides(nz - 1, lambda zz, way: piece(zz))
    xg.sides(nz - 2, lambda zz, way: red.middle(zz))
    yg.hop(1)
    pg.hop(1)
    xg.sides(nz - 1, lambda zz, way: red.middle(zz))

    def body(h, carry):
        yg.hop(h)
        pg.hop(h)
        return carry

    lax.fori_loop(2, nz, body, 0)
    xg.finish()
    lax.fori_loop(0, nz, lambda i, c: (red.end(i), c)[1], 0)
    yg.finish()
    pg.finish()
    lax.fori_loop(1, n, lambda i, c: (row(i, me).wait_send(), c)[1], 0)

    quarter = nt // n_ga
    weight = v_ref[...].reshape(1, width)

    def source(a, carry):
        both = []
        for r in range(CAPQ):
            k = tab[a, me * CAPQ + r] + a * per_dev
            k2 = jnp.maximum(tab[a, 2 * slots + me * CAPQ + r], 0)
            direct = lax.dot_general(half[a * CAPQ + r], y_all[k2], DIMS, preferred_element_type=F32)
            weighted = p_all[k].astype(F32) * weight
            high = weighted.astype(BF16)
            low = (weighted - high.astype(F32)).astype(BF16)
            other = p_all[k2]
            term = lax.dot_general(high, other, DIMS, preferred_element_type=F32)
            term += lax.dot_general(low, other, DIMS, preferred_element_type=F32)
            both.append(2.0 * term - direct)
        v = jnp.concatenate(both, axis=1)
        for i in range(n_ga):
            part2[i, a] = v[i * quarter : (i + 1) * quarter]
        return carry

    lax.fori_loop(0, n, source, 0)
    end = Reduce(part2, own, q1, qt, q2, t1, u1, t2, u2, n)
    end.begin(0)
    shape = own.shape[1:]
    left = lax.broadcasted_iota(I32, shape, 1) < nt

    def seconds(a, carry):
        at = 2 * slots + me * CAPQ
        second[a] = jnp.where(left, tab[a, at], tab[a, at + 1])
        return carry

    lax.fori_loop(0, n, seconds, 0)
    end.middle(0)
    end.end(0)
    doubles = per_dev // 2

    def fill(b, carry):
        outbox[b, 0] = own[b]

        def add(a, sums):
            out = []
            for i in range(per_dev):
                out.append(sums[i] + jnp.where(second[a] == b * per_dev + i, own[a], 0.0))
            return tuple(out)

        sums = lax.fori_loop(0, n, add, tuple(jnp.zeros(shape, F32) for _ in range(per_dev)))
        sums = [v[:, :nt] + v[:, nt:] for v in sums]
        for i in range(doubles):
            outbox[b, 1 + i] = jnp.concatenate([sums[i], sums[i + doubles]], axis=1)
        return carry

    lax.fori_loop(0, n, fill, 0)

    def cross(i, whose):
        to = lax.rem(me + i, n)
        return remote(outbox.at[to], inbox.at[whose], as_.at[i], ar.at[whose], {"ka": to})

    lax.fori_loop(1, n, lambda i, c: (cross(i, me).start(), c)[1], 0)
    inbox[me] = outbox[me]
    lax.fori_loop(1, n, lambda i, c: (cross(i, lax.rem(me + n - i, n)).wait_recv(), c)[1], 0)
    lax.fori_loop(1, n, lambda i, c: (cross(i, me).wait_send(), c)[1], 0)

    sub = quarter // 2
    for j in range(rows):
        at = at_ref[j]
        o, r = at // CAPQ, at % CAPQ
        even = inbox[o, 0, pl.ds(0, sub, stride=2)]
        odd = inbox[o, 0, pl.ds(1, sub, stride=2)]
        zero = jnp.concatenate([even[:, :nt], odd[:, :nt]], axis=1)
        one = jnp.concatenate([even[:, nt:], odd[:, nt:]], axis=1)
        lines[g, pl.ds(j * sub, sub)] = jnp.where(r == 0, zero, one)
    base = rows * sub
    for i in range(doubles):
        total = lax.fori_loop(
            1, n, lambda o, t, i=i: t + inbox[o, 1 + i], inbox[0, 1 + i]
        )
        lines[g, pl.ds(base + i * quarter, quarter)] = total
    x, c = g // 2, g % 2
    mate, far = x * 2 + 1 - c, (1 - x) * 2 + c

    def spread(i, whose, to):
        return remote(lines.at[whose], lines.at[whose], gs.at[i], gr.at[i], {"ga": to})

    spread(0, g, far).start()
    spread(1, g, mate).start()
    spread(0, far, far).wait_recv()
    spread(2, far, mate).start()
    spread(1, mate, mate).wait_recv()
    spread(2, (1 - x) * 2 + 1 - c, mate).wait_recv()
    spread(0, g, far).wait_send()
    spread(1, g, mate).wait_send()
    spread(2, far, mate).wait_send()

    lanes = 2 * nt
    for q in range(n_ga):
        for t in range(sub):
            blocks_ref[:, (q * sub + t) * lanes : (q * sub + t + 1) * lanes] = lines[
                q, pl.ds(t, rows, stride=sub)
            ]
    for i in range(doubles):
        whole = jnp.concatenate(
            [lines[q, pl.ds(base + i * quarter, quarter)] for q in range(n_ga)], axis=0
        )
        turned[...] = whole.T
        even = turned[pl.ds(0, nt, stride=2)]
        odd = turned[pl.ds(1, nt, stride=2)]
        both = jnp.concatenate([even, odd], axis=1)
        flat[pl.ds(i * nt // 2, nt // 2)] = both[: nt // 2]
        flat[pl.ds((i + doubles) * nt // 2, nt // 2)] = both[nt // 2 :]
    for t in range(nt // 2):
        mirr_ref[:, t * lanes : (t + 1) * lanes] = flat[pl.ds(t, per_dev, stride=nt // 2)]


def per_device(x_dens, y_dens, p_dens, coulomb, screened, pairs, q_slot):
    n = lax.axis_size("ka")
    n_ga = lax.axis_size("ga")
    per_dev, nt, g = x_dens.shape
    q_slots = screened.shape[0]
    rows = pairs.shape[0]
    slots = n * CAPQ
    nz = n // 2
    shape = jax.ShapeDtypeStruct
    wide = F32 if slots * nt <= 2048 else BF16
    quarter = nt // n_ga
    each = (quarter, CAPQ * nt)
    line = (n,) + each
    dma = lambda m: pltpu.SemaphoreType.DMA((m,))
    row_len = -(-3 * slots // 128) * 128
    k_all = n * per_dev
    blocks, mirrored = pl.pallas_call(
        functools.partial(kernel, n),
        out_shape=[shape((rows, nt * nt), F32), shape((per_dev, nt * nt), F32)],
        in_specs=[SM, SM, VM, VM, VM, VM, HB],
        out_specs=[VM, VM],
        scratch_shapes=[
            pltpu.SMEM((n, row_len), I32),
            pltpu.SMEM((rows,), I32),
            pltpu.SMEM((3, rows), I32),
            pltpu.VMEM((g, q_slots, screened.shape[2]), BF16),
            pltpu.VMEM((q_slots, g, screened.shape[2]), BF16),
            pltpu.VMEM((nz * per_dev, nt, g), BF16),
            pltpu.VMEM((nz * CAPQ, nt, g), BF16),
            pltpu.VMEM((nz * CAPQ, nt, g), BF16),
            pltpu.VMEM((k_all, nt, g), BF16),
            pltpu.VMEM((k_all, nt, g), BF16),
            pltpu.VMEM((n_ga, slots, nt, g), wide),
            pltpu.VMEM((slots, nt, g), BF16),
            pltpu.VMEM((2, slots, nt, g), wide),
            pltpu.VMEM((slots, nt, g), BF16),
            pltpu.VMEM((slots, nt, g), BF16),
            pltpu.VMEM((n_ga,) + line, F32),
            pltpu.VMEM(line, F32),
            pltpu.VMEM((2,) + line, F32),
            pltpu.VMEM(line, F32),
            pltpu.VMEM(line, F32),
            pltpu.VMEM(line, I32),
            pltpu.VMEM((n, 1 + per_dev // 2) + each, F32),
            pltpu.VMEM((n, 1 + per_dev // 2) + each, F32),
            pltpu.VMEM((n_ga, rows * quarter // 2 + per_dev // 2 * quarter, CAPQ * nt), F32),
            pltpu.VMEM((2 * nt, nt), F32),
            pltpu.VMEM((per_dev * nt // 2, 2 * nt), F32),
            pltpu.SemaphoreType.DMA,
            dma(n), dma(n),
            dma(2 * nz * per_dev), dma(nz * per_dev),
            dma(nz), dma(nz),
            dma(3 * k_all), dma(k_all),
            dma(3 * k_all), dma(k_all),
            dma(2 * nz), dma(2 * nz), dma(nz), dma(nz),
            dma(2), dma(2), dma(1), dma(1),
            dma(n), dma(n),
            dma(3), dma(3),
        ],
        compiler_params=pltpu.CompilerParams(
            collective_id=0, has_side_effects=True, vmem_limit_bytes=LIMIT
        ),
        name="window",
    )(pairs.T, q_slot, x_dens, y_dens, p_dens, coulomb, screened.transpose(1, 0, 2))
    return (blocks, mirrored)


def solution(mesh):
    in_specs = (
        P("ka", None, "ga"),
        P("ka", None, "ga"),
        P("ka", None, "ga"),
        P("ga"),
        P("ka", "ga", None),
        P("ka", None),
        P(),
    )
    out_specs = (P("ka", None), P("ka", None))
    return jax.shard_map(
        per_device, mesh=mesh, in_specs=in_specs, out_specs=out_specs, check_vma=False
    )
```

time: 116 us -> 81.1 us (0.70); the launches traced: 114 us -> 80.9 us
  Pallas kernels: 102 us -> 77.1 us
  local copies, waits for them, and re-layouts: 11.2 us -> 3.14 us
    pallas_call x5 -> x1, Pallas kernels: 102 us -> 77.1 us  [per_device(): pl.pallas_call(functools.partial(kernel, n), out_shape=[shape((rows, nt *...]
    reshape x5 -> x0, local copies, waits for them, and re-layouts: 4.75 us -> none  [the longest x1 1.62 us: per_device(): listed = listed.reshape(n * rows, 128)[:, :3].reshape(n * rows * 3)]
    slice x2 -> x0, local copies, waits for them, and re-layouts: 2.16 us -> none  [per_device(): split = lambda v: jnp.concatenate([v[..., :nt], v[..., nt:]], axis=1)]
    unnamed x4 -> x2, local copies, waits for them, and re-layouts: 4.04 us -> 3.14 us
where the time goes in v1:
time: 81.1 us; the launch traced here: 80.9 us
  Pallas kernels  77.1 us (95%)
  local copies, waits for them, and re-layouts  3.14 us (4%)
    pallas_call x1, Pallas kernels, per_device(): pl.pallas_call(functools.partial(kernel, n), out_shape=[shape((rows, nt *...  77.1 us
    unnamed x2, local copies, waits for them, and re-layouts  3.14 us

profile of v1, /device:TPU:0, one launch (start us, length us, event | category | flops | bytes accessed | tf_op | source)
XLA Modules:
  0.0 80.9 jit_solution(17483981812404852829)
XLA Ops:
  0.6 77.1 %window.1 = (f32[16,4096]{1,0:T(8,128)}, f32[4,4096]{1,0:T(4,128)}) custom-call(s32[3,16]{1,0:T(4,128)} %bitcast.3, s32[16]{0:T(128)} %qs_ref.1, bf16[4,64,375]{2,1,0:T(8,128)(2,1)} %x_ref.1, bf16[4,64,375]{2,1,0:T(8,128)(2,1)} %y_ref.1, bf16[4,64,375]{2,1,0:T(8,128)(2,1)} %p_ref.1, f32[375]{0:T(512)} %v_ref.1, bf16[375,2,1500]{2,1,0:T(2,128)(2,1)} %bitcast.2), custom_call_target="tpu_custom_call" | custom-call | tf_op jit(solution)/shard_map/window/pallas_call | solution.py:552
  77.7 1.7 %copy.11 = f32[16,4096]{1,0:T(8,128)} copy(f32[16,4096]{1,0:T(8,128)} %get-tuple-element.4) | data formatting | bytes 524288
  79.4 1.5 %copy.12 = f32[4,4096]{1,0:T(4,128)} copy(f32[4,4096]{1,0:T(4,128)} %get-tuple-element.5) | data formatting | bytes 131072

commit v2 on v1

--- a/solution.py
+++ b/solution.py
@@ -91,6 +91,8 @@
             self.copy(self.z, self.y, k, 2, True).start()
         for k in range(self.size):
             self.chain(self.z, self.y, k, start, own=True)
+
+    def late(self):
         for k in range(self.cut):
             self.copy(self.z, self.y, k, 2, True).start()
         self.out[pl.ds(self.me * self.size, self.size)] = self.src[...]
@@ -150,6 +152,74 @@
         lax.fori_loop(1, self.nz, tail, 0)
 
 
+class Hub(Gather):
+    def __init__(self, n, src, out, send, recv):
+        super().__init__(n, src, out, send, recv, src.shape[0])
+        self.inner = jnp.logical_and(self.z >= 1, self.z <= self.nz - 2)
+        self.edged = jnp.logical_or(self.z == 1, self.z == self.nz - 2)
+        self.edge = jnp.where(self.z == 1, 0, self.nz - 1)
+
+    def chain(self, zz, yy, k, act, ways=(0, 1), own=False):
+        for way in ways:
+            free = self.z <= self.nz - 3 if way == 0 else self.z >= 2
+
+            @pl.when(free)
+            def _(way=way):
+                act(self.copy(zz, yy, k, way, own))
+
+    def first(self):
+        for k in range(self.size):
+            self.chain(self.z, self.y, k, start, own=True)
+
+        @pl.when(self.inner)
+        def _():
+            for k in range(self.size):
+                self.copy(self.z, self.y, k, 2, True).start()
+
+        self.out[pl.ds(self.me * self.size, self.size)] = self.src[...]
+
+    def hop(self, h):
+        def own(zz, way):
+            last = jnp.logical_and(self.edged, zz == self.edge)
+            for k in range(self.size):
+                self.copy(zz, self.y, k, 2).wait_recv()
+                self.chain(zz, self.y, k, start, (way,))
+
+                @pl.when(last)
+                def _(k=k):
+                    self.copy(zz, self.y, k, 2).start()
+
+        @pl.when(self.inner)
+        def _():
+            self.sides(h, own)
+
+    def finish(self):
+        for k in range(self.size):
+            self.chain(self.z, self.y, k, sent, own=True)
+
+        @pl.when(self.inner)
+        def _():
+            for k in range(self.size):
+                self.copy(self.z, self.y, k, 2, True).wait_send()
+                self.copy(self.z, 1 - self.y, k, 2).wait_recv()
+
+            @pl.when(self.edged)
+            def _():
+                for k in range(self.size):
+                    self.copy(self.edge, self.y, k, 2).wait_send()
+                    self.copy(self.edge, 1 - self.y, k, 2).wait_recv()
+
+            def tail(h, carry):
+                def side(zz, way):
+                    for k in range(self.size):
+                        self.chain(zz, self.y, k, sent, (way,))
+
+                self.sides(h, side)
+                return carry
+
+            lax.fori_loop(1, self.nz, tail, 0)
+
+
 class Pick:
     def __init__(self, n, src, col, out, got, tab, send, recv, ps, pr):
         self.n, self.nz = n, n // 2
@@ -298,27 +368,28 @@
     me = lax.axis_index("ka")
     rows = pairs_ref.shape[1]
     slots = n * CAPQ
-    owners = []
+    holders = ([], [])
     for j in range(rows):
         slot = qs_ref[pairs_ref[2, j]]
         owner = slot // q_slots
-        rank = jnp.int32(0)
-        for o in owners:
-            rank = rank + jnp.where(o == owner, 1, 0)
-        owners.append(owner)
-        at_ref[j] = owner * CAPQ + rank
-        kept[0, j] = pairs_ref[0, j] - me * per_dev
+        kept[0, j] = pairs_ref[0, j] % per_dev
         kept[1, j] = slot - owner * q_slots
         kept[2, j] = pairs_ref[1, j]
+        for i, o in enumerate((owner, pairs_ref[1, j] // per_dev)):
+            rank = jnp.int32(0)
+            for other in holders[i]:
+                rank = rank + jnp.where(other == o, 1, 0)
+            holders[i].append(o)
+            at_ref[i, j] = o * CAPQ + rank
 
     def one(s, carry):
-        found = [jnp.int32(0), jnp.int32(0), jnp.int32(-1)]
-        for j in range(rows):
-            hit = at_ref[j] == s
-            for i in range(3):
-                found[i] = jnp.where(hit, kept[i, j], found[i])
-        for i in range(3):
-            tab[me, i * slots + s] = found[i]
+        for i, which in ((0, (0, 1, 2)), (1, (0, 2))):
+            found = [jnp.int32(-1 if w == 2 else 0) for w in which]
+            for j in range(rows):
+                hit = at_ref[i, j] == s
+                found = [jnp.where(hit, kept[w, j], f) for w, f in zip(which, found)]
+            for w, f in enumerate(found):
+                tab[me, (3 * i + w) * slots + s] = f
         return carry
 
     lax.fori_loop(0, slots, one, 0)
@@ -327,8 +398,9 @@
 def kernel(n, pairs_ref, qs_ref, x_ref, y_ref, p_ref, v_ref, w_hbm, blocks_ref, mirr_ref,
            tab, at_ref, kept, wt, w_ref, x_col, x_out, x_got, y_all, p_all, part, half,
            recv1, tsend, recv2, part2, own, q1, qt, q2, second, outbox, inbox, lines, turned, flat,
+           split, part3, eown, e1, et, e2, ebox, ein, emir,
            ws, ts, tr, xs, xr, xps, xpr, ys, yr, ps, pr, s1, r1, s2, r2, t1, u1, t2, u2,
-           as_, ar, gs, gr):
+           v1, w1, v2, w2, es, er, fs, fr, as_, ar, gs, gr):
     per_dev, nt, width = x_ref.shape
     rows = pairs_ref.shape[1]
     q_slots = w_ref.shape[0]
@@ -343,8 +415,9 @@
     greet(n)
     xg = Pick(n, x_ref, x_col, x_out, x_got, tab, xs, xr, xps, xpr)
     yg = Gather(n, y_ref, y_all, ys, yr, per_dev - 1)
-    pg = Gather(n, p_ref, p_all, ps, pr, per_dev - 1)
+    pg = Hub(n, p_ref, p_all, ps, pr)
     xg.first()
+    yg.first()
     make_row(n, q_slots, per_dev, pairs_ref, qs_ref, tab, at_ref, kept)
 
     def row(i, whose):
@@ -354,6 +427,7 @@
 
     lax.fori_loop(1, n, lambda i, c: (row(i, me).start(), c)[1], 0)
     xg.pass_on(z)
+    yg.late()
     fetch.wait()
     for s in range(q_slots):
         w_ref[s] = wt[:, s, :]
@@ -374,24 +448,27 @@
         red.begin(zz)
 
     xg.hop(1)
-    yg.first()
+    pg.first()
     lax.fori_loop(
         1, n, lambda i, c: (row(i, lax.rem(me + n - i, n)).wait_recv(), c)[1], 0
     )
     xg.sides(1, lambda zz, way: xg.pass_on(zz))
+    yg.second()
     piece(z)
-    yg.second()
 
     def stage(h, carry):
-        xg.hop(h)
-        xg.sides(h, lambda zz, way: xg.pass_on(zz))
+        @pl.when(h < nz)
+        def _():
+            xg.hop(h)
+            xg.sides(h, lambda zz, way: xg.pass_on(zz))
+
+        yg.hop(h - 1)
+        pg.hop(h - 1)
+        xg.sides(h - 1, lambda zz, way: piece(zz))
 
         @pl.when(h == 2)
         def _():
-            pg.first()
             red.middle(z)
-
-        xg.sides(h - 1, lambda zz, way: piece(zz))
 
         @pl.when(h > 2)
         def _():
@@ -399,45 +476,69 @@
 
         return carry
 
-    lax.fori_loop(2, nz, stage, 0)
-    pg.second()
-    xg.sides(nz - 1, lambda zz, way: piece(zz))
-    xg.sides(nz - 2, lambda zz, way: red.middle(zz))
-    yg.hop(1)
-    pg.hop(1)
+    lax.fori_loop(2, nz + 1, stage, 0)
+    xg.finish()
+    pg.finish()
     xg.sides(nz - 1, lambda zz, way: red.middle(zz))
 
-    def body(h, carry):
-        yg.hop(h)
-        pg.hop(h)
-        return carry
-
-    lax.fori_loop(2, nz, body, 0)
-    xg.finish()
+    quarter = nt // n_ga
+    weight = v_ref[...].reshape(1, width)
+    sets = jnp.where(pg.edged, 4, 2)
+    ered = Reduce(part3, eown, e1, et, e2, v1, w1, v2, w2, 4 * nz)
+
+    def of(q):
+        return jnp.where(q // 2 == 0, z, pg.edge) * 2 + q % 2
+
+    def joined(both, out, at):
+        v = jnp.concatenate(both, axis=1)
+        for i in range(n_ga):
+            out[i, at] = v[i * quarter : (i + 1) * quarter]
+
+    @pl.when(pg.inner)
+    def _():
+        def exchange(q, carry):
+            a = of(q)
+            for k in range(per_dev):
+                weighted = p_all[a * per_dev + k].astype(F32) * weight
+                high = weighted.astype(BF16)
+                split[k, :nt] = high
+                split[k, nt:] = (weighted - high.astype(F32)).astype(BF16)
+
+            def level(zz, carry):
+                both = []
+                for r in range(CAPQ):
+                    at = 3 * slots + (zz * 2 + y) * CAPQ + r
+                    k2 = jnp.maximum(tab[a, at + slots], 0)
+                    v = lax.dot_general(
+                        split[tab[a, at]], p_all[k2], DIMS, preferred_element_type=F32
+                    )
+                    both.append(v[:nt] + v[nt:])
+                joined(both, part3, q * nz + zz)
+                return carry
+
+            lax.fori_loop(0, nz, level, 0)
+            return carry
+
+        lax.fori_loop(0, sets, exchange, 0)
+        ered.begin(0)
+
     lax.fori_loop(0, nz, lambda i, c: (red.end(i), c)[1], 0)
     yg.finish()
-    pg.finish()
+
+    @pl.when(pg.inner)
+    def _():
+        ered.middle(0)
+
     lax.fori_loop(1, n, lambda i, c: (row(i, me).wait_send(), c)[1], 0)
-
-    quarter = nt // n_ga
-    weight = v_ref[...].reshape(1, width)
 
     def source(a, carry):
         both = []
         for r in range(CAPQ):
-            k = tab[a, me * CAPQ + r] + a * per_dev
             k2 = jnp.maximum(tab[a, 2 * slots + me * CAPQ + r], 0)
-            direct = lax.dot_general(half[a * CAPQ + r], y_all[k2], DIMS, preferred_element_type=F32)
-            weighted = p_all[k].astype(F32) * weight
-            high = weighted.astype(BF16)
-            low = (weighted - high.astype(F32)).astype(BF16)
-            other = p_all[k2]
-            term = lax.dot_general(high, other, DIMS, preferred_element_type=F32)
-            term += lax.dot_general(low, other, DIMS, preferred_element_type=F32)
-            both.append(2.0 * term - direct)
-        v = jnp.concatenate(both, axis=1)
-        for i in range(n_ga):
-            part2[i, a] = v[i * quarter : (i + 1) * quarter]
+            both.append(
+                lax.dot_general(half[a * CAPQ + r], y_all[k2], DIMS, preferred_element_type=F32)
+            )
+        joined(both, part2, a)
         return carry
 
     lax.fori_loop(0, n, source, 0)
@@ -445,6 +546,13 @@
     end.begin(0)
     shape = own.shape[1:]
     left = lax.broadcasted_iota(I32, shape, 1) < nt
+    doubles = per_dev // 2
+
+    def paired(sums):
+        sums = [v[:, :nt] + v[:, nt:] for v in sums]
+        return [
+            jnp.concatenate([sums[i], sums[i + doubles]], axis=1) for i in range(doubles)
+        ]
 
     def seconds(a, carry):
         at = 2 * slots + me * CAPQ
@@ -452,9 +560,64 @@
         return carry
 
     lax.fori_loop(0, n, seconds, 0)
+
+    def to_first(q):
+        return remote(
+            eown.at[pl.ds(q * nz, nz)], ein.at[y], es.at[q], er.at[y], {"ka": of(q)}
+        )
+
+    def to_second(zz):
+        return remote(ebox.at[zz], emir.at[z], fs.at[zz], fr.at[z], {"ka": zz * 2 + y})
+
+    def others(act):
+        def one(q, carry):
+            @pl.when(q != y)
+            def _():
+                act(to_first(q))
+
+            return carry
+
+        lax.fori_loop(0, sets, one, 0)
+
+    def levels(act):
+        def one(zz, carry):
+            @pl.when(zz != z)
+            def _():
+                act(to_second(zz))
+
+            return carry
+
+        lax.fori_loop(0, nz, one, 0)
+
+    @pl.when(pg.inner)
+    def _():
+        ered.end(0)
+        others(start)
+        ein[y] = eown[pl.ds(y * nz, nz)]
+
+        def level(zz, carry):
+            def add(q, sums):
+                at = 4 * slots + (zz * 2 + y) * CAPQ
+                k2 = jnp.where(left, tab[of(q), at], tab[of(q), at + 1])
+                v = eown[q * nz + zz]
+                base = (zz * 2 + y) * per_dev
+                return tuple(
+                    t + jnp.where(k2 == base + i, v, 0.0) for i, t in enumerate(sums)
+                )
+
+            sums = lax.fori_loop(
+                0, sets, add, tuple(jnp.zeros(shape, F32) for _ in range(per_dev))
+            )
+            for i, v in enumerate(paired(sums)):
+                ebox[zz, i] = v
+            return carry
+
+        lax.fori_loop(0, nz, level, 0)
+        levels(start)
+        emir[z] = ebox[z]
+
     end.middle(0)
     end.end(0)
-    doubles = per_dev // 2
 
     def fill(b, carry):
         outbox[b, 0] = own[b]
@@ -466,9 +629,8 @@
             return tuple(out)
 
         sums = lax.fori_loop(0, n, add, tuple(jnp.zeros(shape, F32) for _ in range(per_dev)))
-        sums = [v[:, :nt] + v[:, nt:] for v in sums]
-        for i in range(doubles):
-            outbox[b, 1 + i] = jnp.concatenate([sums[i], sums[i + doubles]], axis=1)
+        for i, v in enumerate(paired(sums)):
+            outbox[b, 1 + i] = v
         return carry
 
     lax.fori_loop(0, n, fill, 0)
@@ -479,24 +641,54 @@
 
     lax.fori_loop(1, n, lambda i, c: (cross(i, me).start(), c)[1], 0)
     inbox[me] = outbox[me]
+    for yy in range(2):
+
+        @pl.when(jnp.logical_or(jnp.logical_not(pg.inner), yy != y))
+        def _(yy=yy):
+            remote(ein.at[yy], ein.at[yy], es.at[0], er.at[yy], {"ka": z * 2 + 1 - y}).wait_recv()
+
+    def inner_level(zz, carry):
+        @pl.when(zz != z)
+        def _():
+            remote(
+                emir.at[zz], emir.at[zz], fs.at[0], fr.at[zz], {"ka": z * 2 + 1 - y}
+            ).wait_recv()
+
+        return carry
+
+    lax.fori_loop(1, nz - 1, inner_level, 0)
     lax.fori_loop(1, n, lambda i, c: (cross(i, lax.rem(me + n - i, n)).wait_recv(), c)[1], 0)
     lax.fori_loop(1, n, lambda i, c: (cross(i, me).wait_send(), c)[1], 0)
 
+    @pl.when(pg.inner)
+    def _():
+        others(sent)
+        levels(sent)
+
     sub = quarter // 2
-    for j in range(rows):
-        at = at_ref[j]
-        o, r = at // CAPQ, at % CAPQ
-        even = inbox[o, 0, pl.ds(0, sub, stride=2)]
-        odd = inbox[o, 0, pl.ds(1, sub, stride=2)]
+
+    def picked(ref, at, r):
+        even = ref[at + (pl.ds(0, sub, stride=2),)]
+        odd = ref[at + (pl.ds(1, sub, stride=2),)]
         zero = jnp.concatenate([even[:, :nt], odd[:, :nt]], axis=1)
         one = jnp.concatenate([even[:, nt:], odd[:, nt:]], axis=1)
-        lines[g, pl.ds(j * sub, sub)] = jnp.where(r == 0, zero, one)
+        return jnp.where(r == 0, zero, one)
+
+    for j in range(rows):
+        at, et_ = at_ref[0, j], at_ref[1, j]
+        b = et_ // CAPQ
+        direct = picked(inbox, (at // CAPQ, 0), at % CAPQ)
+        term = picked(ein, (b % 2, b // 2), et_ % CAPQ)
+        lines[g, pl.ds(j * sub, sub)] = 2.0 * term - direct
     base = rows * sub
     for i in range(doubles):
         total = lax.fori_loop(
             1, n, lambda o, t, i=i: t + inbox[o, 1 + i], inbox[0, 1 + i]
         )
-        lines[g, pl.ds(base + i * quarter, quarter)] = total
+        term = lax.fori_loop(
+            2, nz - 1, lambda zz, t, i=i: t + emir[zz, i], emir[1, i]
+        )
+        lines[g, pl.ds(base + i * quarter, quarter)] = 2.0 * term - total
     x, c = g // 2, g % 2
     mate, far = x * 2 + 1 - c, (1 - x) * 2 + c
 
@@ -547,7 +739,7 @@
     each = (quarter, CAPQ * nt)
     line = (n,) + each
     dma = lambda m: pltpu.SemaphoreType.DMA((m,))
-    row_len = -(-3 * slots // 128) * 128
+    row_len = -(-5 * slots // 128) * 128
     k_all = n * per_dev
     blocks, mirrored = pl.pallas_call(
         functools.partial(kernel, n),
@@ -556,7 +748,7 @@
         out_specs=[VM, VM],
         scratch_shapes=[
             pltpu.SMEM((n, row_len), I32),
-            pltpu.SMEM((rows,), I32),
+            pltpu.SMEM((2, rows), I32),
             pltpu.SMEM((3, rows), I32),
             pltpu.VMEM((g, q_slots, screened.shape[2]), BF16),
             pltpu.VMEM((q_slots, g, screened.shape[2]), BF16),
@@ -581,6 +773,15 @@
             pltpu.VMEM((n_ga, rows * quarter // 2 + per_dev // 2 * quarter, CAPQ * nt), F32),
             pltpu.VMEM((2 * nt, nt), F32),
             pltpu.VMEM((per_dev * nt // 2, 2 * nt), F32),
+            pltpu.VMEM((per_dev, 2 * nt, g), BF16),
+            pltpu.VMEM((n_ga, 4 * nz) + each, F32),
+            pltpu.VMEM((4 * nz,) + each, F32),
+            pltpu.VMEM((2, 4 * nz) + each, F32),
+            pltpu.VMEM((4 * nz,) + each, F32),
+            pltpu.VMEM((4 * nz,) + each, F32),
+            pltpu.VMEM((nz, per_dev // 2) + each, F32),
+            pltpu.VMEM((2, nz) + each, F32),
+            pltpu.VMEM((nz, per_dev // 2) + each, F32),
             pltpu.SemaphoreType.DMA,
             dma(n), dma(n),
             dma(2 * nz * per_dev), dma(nz * per_dev),
@@ -589,6 +790,8 @@
             dma(3 * k_all), dma(k_all),
             dma(2 * nz), dma(2 * nz), dma(nz), dma(nz),
             dma(2), dma(2), dma(1), dma(1),
+            dma(2), dma(2), dma(1), dma(1),
+            dma(4), dma(2), dma(nz), dma(nz),
             dma(n), dma(n),
             dma(3), dma(3),
         ],

time: 81.1 us -> 77.8 us (0.959)
  Pallas kernels: 77.1 us -> 73.8 us
    pallas_call x1, Pallas kernels: 77.1 us -> 73.8 us  [per_device(): pl.pallas_call(functools.partial(kernel, n), out_shape=[shape((rows, nt *...]
where the time goes in v2:
time: 77.8 us; the launch traced here: 77.6 us
  Pallas kernels  73.8 us (95%)
  local copies, waits for them, and re-layouts  3.14 us (4%)
    pallas_call x1, Pallas kernels, per_device(): pl.pallas_call(functools.partial(kernel, n), out_shape=[shape((rows, nt *...  73.8 us
    unnamed x2, local copies, waits for them, and re-layouts  3.14 us

profile of v2, /device:TPU:0, one launch (start us, length us, event | category | flops | bytes accessed | tf_op | source)
XLA Modules:
  0.0 77.6 jit_solution(5511519347387940288)
XLA Ops:
  0.6 73.8 %window.1 = (f32[16,4096]{1,0:T(8,128)}, f32[4,4096]{1,0:T(4,128)}) custom-call(s32[3,16]{1,0:T(4,128)} %bitcast.3, s32[16]{0:T(128)} %qs_ref.1, bf16[4,64,375]{2,1,0:T(8,128)(2,1)} %x_ref.1, bf16[4,64,375]{2,1,0:T(8,128)(2,1)} %y_ref.1, bf16[4,64,375]{2,1,0:T(8,128)(2,1)} %p_ref.1, f32[375]{0:T(512)} %v_ref.1, bf16[375,2,1500]{2,1,0:T(2,128)(2,1)} %bitcast.2), custom_call_target="tpu_custom_call" | custom-call | tf_op jit(solution)/shard_map/window/pallas_call | solution.py:744
  74.4 1.7 %copy.11 = f32[16,4096]{1,0:T(8,128)} copy(f32[16,4096]{1,0:T(8,128)} %get-tuple-element.4) | data formatting | bytes 524288
  76.1 1.5 %copy.12 = f32[4,4096]{1,0:T(4,128)} copy(f32[4,4096]{1,0:T(4,128)} %get-tuple-element.5) | data formatting | bytes 131072

commit v3 on v2

--- a/solution.py
+++ b/solution.py
@@ -86,16 +86,14 @@
     def early(self):
         return range(self.cut, self.size)
 
+    def across(self):
+        for k in reversed(range(self.size)):
+            self.copy(self.z, self.y, k, 2, True).start()
+        self.out[pl.ds(self.me * self.size, self.size)] = self.src[...]
+
     def first(self):
-        for k in self.early():
-            self.copy(self.z, self.y, k, 2, True).start()
         for k in range(self.size):
             self.chain(self.z, self.y, k, start, own=True)
-
-    def late(self):
-        for k in range(self.cut):
-            self.copy(self.z, self.y, k, 2, True).start()
-        self.out[pl.ds(self.me * self.size, self.size)] = self.src[...]
 
     def second(self):
         for k in self.early():
@@ -364,42 +362,38 @@
         self.two(i).wait_send()
 
 
-def make_row(n, q_slots, per_dev, pairs_ref, qs_ref, tab, at_ref, kept):
-    me = lax.axis_index("ka")
+def make_row(n, q_slots, per_dev, pairs_ref, qs_ref, row_ref, at_ref):
     rows = pairs_ref.shape[1]
     slots = n * CAPQ
+    lane = lax.broadcasted_iota(I32, row_ref.shape, 1)
+    section = lane // slots
+    spot = lane % slots
+    row = jnp.where(jnp.logical_or(section == 2, section == 4), -1, 0)
     holders = ([], [])
     for j in range(rows):
         slot = qs_ref[pairs_ref[2, j]]
         owner = slot // q_slots
-        kept[0, j] = pairs_ref[0, j] % per_dev
-        kept[1, j] = slot - owner * q_slots
-        kept[2, j] = pairs_ref[1, j]
-        for i, o in enumerate((owner, pairs_ref[1, j] // per_dev)):
+        first, second = pairs_ref[0, j] % per_dev, pairs_ref[1, j]
+        at = []
+        for i, o in enumerate((owner, second // per_dev)):
             rank = jnp.int32(0)
             for other in holders[i]:
                 rank = rank + jnp.where(other == o, 1, 0)
             holders[i].append(o)
-            at_ref[i, j] = o * CAPQ + rank
-
-    def one(s, carry):
-        for i, which in ((0, (0, 1, 2)), (1, (0, 2))):
-            found = [jnp.int32(-1 if w == 2 else 0) for w in which]
-            for j in range(rows):
-                hit = at_ref[i, j] == s
-                found = [jnp.where(hit, kept[w, j], f) for w, f in zip(which, found)]
-            for w, f in enumerate(found):
-                tab[me, (3 * i + w) * slots + s] = f
-        return carry
-
-    lax.fori_loop(0, slots, one, 0)
-
-
-def kernel(n, pairs_ref, qs_ref, x_ref, y_ref, p_ref, v_ref, w_hbm, blocks_ref, mirr_ref,
-           tab, at_ref, kept, wt, w_ref, x_col, x_out, x_got, y_all, p_all, part, half,
-           recv1, tsend, recv2, part2, own, q1, qt, q2, second, outbox, inbox, lines, turned, flat,
+            at.append(o * CAPQ + rank)
+            at_ref[i, j] = at[i]
+        value = jnp.where(section == 1, slot - owner * q_slots, second)
+        value = jnp.where(jnp.logical_or(section == 0, section == 3), first, value)
+        hit = spot == jnp.where(section < 3, at[0], at[1])
+        row = jnp.where(hit, value, row)
+    row_ref[...] = row
+
+
+def kernel(n, pairs_ref, qs_ref, x_ref, y_ref, p_ref, v_ref, w_hbm, lines,
+           tab, at_ref, row_ref, wt, w_ref, x_col, x_out, x_got, y_all, p_all, part, half,
+           recv1, tsend, recv2, part2, own, q1, qt, q2, second, outbox, inbox,
            split, part3, eown, e1, et, e2, ebox, ein, emir,
-           ws, ts, tr, xs, xr, xps, xpr, ys, yr, ps, pr, s1, r1, s2, r2, t1, u1, t2, u2,
+           ws, ls, ts, tr, xs, xr, xps, xpr, ys, yr, ps, pr, s1, r1, s2, r2, t1, u1, t2, u2,
            v1, w1, v2, w2, es, er, fs, fr, as_, ar, gs, gr):
     per_dev, nt, width = x_ref.shape
     rows = pairs_ref.shape[1]
@@ -417,20 +411,31 @@
     yg = Gather(n, y_ref, y_all, ys, yr, per_dev - 1)
     pg = Hub(n, p_ref, p_all, ps, pr)
     xg.first()
-    yg.first()
-    make_row(n, q_slots, per_dev, pairs_ref, qs_ref, tab, at_ref, kept)
+    make_row(n, q_slots, per_dev, pairs_ref, qs_ref, row_ref, at_ref)
+    keep = pltpu.make_async_copy(row_ref.at[0], tab.at[me], ls)
+    keep.start()
 
     def row(i, whose):
         return remote(
-            tab.at[whose], tab.at[whose], ts.at[i], tr.at[whose], {"ka": lax.rem(me + i, n)}
+            row_ref.at[0], tab.at[whose], ts.at[i], tr.at[whose], {"ka": lax.rem(me + i, n)}
         )
 
     lax.fori_loop(1, n, lambda i, c: (row(i, me).start(), c)[1], 0)
+    keep.wait()
     xg.pass_on(z)
-    yg.late()
+    yg.across()
     fetch.wait()
-    for s in range(q_slots):
-        w_ref[s] = wt[:, s, :]
+    turn = 16
+    whole = width // turn * turn
+
+    def relay(i, carry):
+        at = pl.ds(pl.multiple_of(i * turn, turn), turn)
+        w_ref[:, at] = jnp.swapaxes(wt[at], 0, 1)
+        return carry
+
+    lax.fori_loop(0, width // turn, relay, 0)
+    if whole < width:
+        w_ref[:, whole:] = jnp.swapaxes(wt[whole:], 0, 1)
     red = Reduce(part, half, recv1, tsend, recv2, s1, r1, s2, r2, 2 * CAPQ)
 
     def multiply(v, a, r):
@@ -448,22 +453,30 @@
         red.begin(zz)
 
     xg.hop(1)
-    pg.first()
     lax.fori_loop(
         1, n, lambda i, c: (row(i, lax.rem(me + n - i, n)).wait_recv(), c)[1], 0
     )
     xg.sides(1, lambda zz, way: xg.pass_on(zz))
-    yg.second()
     piece(z)
 
     def stage(h, carry):
         @pl.when(h < nz)
         def _():
             xg.hop(h)
+
+        @pl.when(h == 2)
+        def _():
+            yg.first()
+            pg.first()
+
+        @pl.when(h < nz)
+        def _():
             xg.sides(h, lambda zz, way: xg.pass_on(zz))
 
-        yg.hop(h - 1)
-        pg.hop(h - 1)
+        @pl.when(h == 2)
+        def _():
+            yg.second()
+
         xg.sides(h - 1, lambda zz, way: piece(zz))
 
         @pl.when(h == 2)
@@ -473,13 +486,17 @@
         @pl.when(h > 2)
         def _():
             xg.sides(h - 2, lambda zz, way: red.middle(zz))
+            yg.hop(h - 2)
+            pg.hop(h - 2)
 
         return carry
 
     lax.fori_loop(2, nz + 1, stage, 0)
+    xg.sides(nz - 1, lambda zz, way: red.middle(zz))
+    yg.hop(nz - 1)
+    pg.hop(nz - 1)
     xg.finish()
     pg.finish()
-    xg.sides(nz - 1, lambda zz, way: red.middle(zz))
 
     quarter = nt // n_ga
     weight = v_ref[...].reshape(1, width)
@@ -541,7 +558,7 @@
         joined(both, part2, a)
         return carry
 
-    lax.fori_loop(0, n, source, 0)
+    lax.fori_loop(0, n, source, 0, unroll=2)
     end = Reduce(part2, own, q1, qt, q2, t1, u1, t2, u2, n)
     end.begin(0)
     shape = own.shape[1:]
@@ -628,7 +645,8 @@
                 out.append(sums[i] + jnp.where(second[a] == b * per_dev + i, own[a], 0.0))
             return tuple(out)
 
-        sums = lax.fori_loop(0, n, add, tuple(jnp.zeros(shape, F32) for _ in range(per_dev)))
+        sums = tuple(jnp.zeros(shape, F32) for _ in range(per_dev))
+        sums = lax.fori_loop(0, n, add, sums, unroll=min(n, 8))
         for i, v in enumerate(paired(sums)):
             outbox[b, 1 + i] = v
         return carry
@@ -705,6 +723,13 @@
     spread(1, g, mate).wait_send()
     spread(2, far, mate).wait_send()
 
+
+def layout(lines, blocks_ref, mirr_ref, turned, flat):
+    n_ga = lines.shape[0]
+    rows, per_dev = blocks_ref.shape[0], mirr_ref.shape[0]
+    nt = turned.shape[1]
+    quarter, sub, doubles = nt // n_ga, nt // n_ga // 2, per_dev // 2
+    base = rows * sub
     lanes = 2 * nt
     for q in range(n_ga):
         for t in range(sub):
@@ -741,15 +766,15 @@
     dma = lambda m: pltpu.SemaphoreType.DMA((m,))
     row_len = -(-5 * slots // 128) * 128
     k_all = n * per_dev
-    blocks, mirrored = pl.pallas_call(
+    lines = pl.pallas_call(
         functools.partial(kernel, n),
-        out_shape=[shape((rows, nt * nt), F32), shape((per_dev, nt * nt), F32)],
+        out_shape=shape((n_ga, rows * quarter // 2 + per_dev // 2 * quarter, CAPQ * nt), F32),
         in_specs=[SM, SM, VM, VM, VM, VM, HB],
-        out_specs=[VM, VM],
+        out_specs=VM,
         scratch_shapes=[
             pltpu.SMEM((n, row_len), I32),
             pltpu.SMEM((2, rows), I32),
-            pltpu.SMEM((3, rows), I32),
+            pltpu.VMEM((1, row_len), I32),
             pltpu.VMEM((g, q_slots, screened.shape[2]), BF16),
             pltpu.VMEM((q_slots, g, screened.shape[2]), BF16),
             pltpu.VMEM((nz * per_dev, nt, g), BF16),
@@ -770,9 +795,6 @@
             pltpu.VMEM(line, I32),
             pltpu.VMEM((n, 1 + per_dev // 2) + each, F32),
             pltpu.VMEM((n, 1 + per_dev // 2) + each, F32),
-            pltpu.VMEM((n_ga, rows * quarter // 2 + per_dev // 2 * quarter, CAPQ * nt), F32),
-            pltpu.VMEM((2 * nt, nt), F32),
-            pltpu.VMEM((per_dev * nt // 2, 2 * nt), F32),
             pltpu.VMEM((per_dev, 2 * nt, g), BF16),
             pltpu.VMEM((n_ga, 4 * nz) + each, F32),
             pltpu.VMEM((4 * nz,) + each, F32),
@@ -782,6 +804,7 @@
             pltpu.VMEM((nz, per_dev // 2) + each, F32),
             pltpu.VMEM((2, nz) + each, F32),
             pltpu.VMEM((nz, per_dev // 2) + each, F32),
+            pltpu.SemaphoreType.DMA,
             pltpu.SemaphoreType.DMA,
             dma(n), dma(n),
             dma(2 * nz * per_dev), dma(nz * per_dev),
@@ -800,6 +823,17 @@
         ),
         name="window",
     )(pairs.T, q_slot, x_dens, y_dens, p_dens, coulomb, screened.transpose(1, 0, 2))
+    blocks, mirrored = pl.pallas_call(
+        layout,
+        out_shape=[shape((rows, nt * nt), F32), shape((per_dev, nt * nt), F32)],
+        in_specs=[VM],
+        out_specs=[VM, VM],
+        scratch_shapes=[
+            pltpu.VMEM((2 * nt, nt), F32),
+            pltpu.VMEM((per_dev * nt // 2, 2 * nt), F32),
+        ],
+        name="layout",
+    )(lines)
     return (blocks, mirrored)
 
 

time: 77.8 us -> 71.3 us (0.916)
  Pallas kernels: 73.8 us -> 70.5 us
  local copies, waits for them, and re-layouts: 3.14 us -> 0 us
    pallas_call x1 -> x2, Pallas kernels: 73.8 us -> 70.5 us  [the longest x1 68.6 us: per_device(): pl.pallas_call(functools.partial(kernel, n), out_shape=shape((n_ga, rows...]
    unnamed x2 -> x0, local copies, waits for them, and re-layouts: 3.14 us -> none
where the time goes in v3:
time: 71.3 us; the launch traced here: 71.2 us
  Pallas kernels  70.5 us (99%)
    pallas_call x1, Pallas kernels, per_device(): pl.pallas_call(functools.partial(kernel, n), out_shape=shape((n_ga, rows...  68.6 us
    pallas_call x1, Pallas kernels, per_device(): pl.pallas_call(layout, out_shape=[shape((rows, nt * nt), F32), shape((per...  1.91 us

profile of v3, /device:TPU:0, one launch (start us, length us, event | category | flops | bytes accessed | tf_op | source)
XLA Modules:
  0.0 71.2 jit_solution(15155073079321374848)
XLA Ops:
  0.6 68.6 %window.1.lines = f32[4,160,128]{2,1,0:T(8,128)} custom-call(s32[3,16]{1,0:T(4,128)} %bitcast.3, s32[16]{0:T(128)} %qs_ref.1, bf16[4,64,375]{2,1,0:T(8,128)(2,1)} %x_ref.1, bf16[4,64,375]{2,1,0:T(8,128)(2,1)} %y_ref.1, bf16[4,64,375]{2,1,0:T(8,128)(2,1)} %p_ref.1, f32[375]{0:T(512)} %v_ref.1, bf16[375,2,1500]{2,1,0:T(2,128)(2,1)} %bitcast.2), custom_call_target="tpu_custom_call" | custom-call | tf_op jit(solution)/shard_map/window/pallas_call | solution.py:769
  69.3 1.9 %layout.1 = (f32[16,4096]{1,0:T(8,128)}, f32[4,4096]{1,0:T(4,128)}) custom-call(f32[4,160,128]{2,1,0:T(8,128)} %window.1.lines), custom_call_target="tpu_custom_call" | custom-call | tf_op jit(solution)/shard_map/layout/pallas_call | solution.py:826

commit v4 on v3

--- a/solution.py
+++ b/solution.py
@@ -86,8 +86,12 @@
     def early(self):
         return range(self.cut, self.size)
 
-    def across(self):
-        for k in reversed(range(self.size)):
+    def across_early(self):
+        for k in self.early():
+            self.copy(self.z, self.y, k, 2, True).start()
+
+    def across_late(self):
+        for k in range(self.cut):
             self.copy(self.z, self.y, k, 2, True).start()
         self.out[pl.ds(self.me * self.size, self.size)] = self.src[...]
 
@@ -168,28 +172,34 @@
     def first(self):
         for k in range(self.size):
             self.chain(self.z, self.y, k, start, own=True)
-
-        @pl.when(self.inner)
-        def _():
-            for k in range(self.size):
-                self.copy(self.z, self.y, k, 2, True).start()
-
         self.out[pl.ds(self.me * self.size, self.size)] = self.src[...]
+
+    def across(self):
+        for k in range(self.size):
+            self.copy(self.z, self.y, k, 2, True).start()
+
+    def onward(self, zz, way):
+        last = jnp.logical_and(self.edged, zz == self.edge)
+        free = self.z <= self.nz - 3 if way == 0 else self.z >= 2
+        return jnp.logical_or(last, free)
 
     def hop(self, h):
         def own(zz, way):
-            last = jnp.logical_and(self.edged, zz == self.edge)
+            on = self.onward(zz, way)
+
+            @pl.when(on)
+            def _():
+                for k in range(self.size):
+                    self.copy(zz, self.y, k, 2).wait_recv()
+                    self.chain(zz, self.y, k, start, (way,))
+
+        self.sides(h, own)
+
+    def across_edge(self):
+        @pl.when(self.edged)
+        def _():
             for k in range(self.size):
-                self.copy(zz, self.y, k, 2).wait_recv()
-                self.chain(zz, self.y, k, start, (way,))
-
-                @pl.when(last)
-                def _(k=k):
-                    self.copy(zz, self.y, k, 2).start()
-
-        @pl.when(self.inner)
-        def _():
-            self.sides(h, own)
+                self.copy(self.edge, self.y, k, 2).start()
 
     def finish(self):
         for k in range(self.size):
@@ -209,8 +219,13 @@
 
             def tail(h, carry):
                 def side(zz, way):
+                    on = self.onward(zz, way)
                     for k in range(self.size):
                         self.chain(zz, self.y, k, sent, (way,))
+
+                        @pl.when(jnp.logical_not(on))
+                        def _(k=k):
+                            self.copy(zz, self.y, k, 2).wait_recv()
 
                 self.sides(h, side)
                 return carry
@@ -410,6 +425,7 @@
     xg = Pick(n, x_ref, x_col, x_out, x_got, tab, xs, xr, xps, xpr)
     yg = Gather(n, y_ref, y_all, ys, yr, per_dev - 1)
     pg = Hub(n, p_ref, p_all, ps, pr)
+    outer = jnp.logical_not(pg.inner)
     xg.first()
     make_row(n, q_slots, per_dev, pairs_ref, qs_ref, row_ref, at_ref)
     keep = pltpu.make_async_copy(row_ref.at[0], tab.at[me], ls)
@@ -423,7 +439,19 @@
     lax.fori_loop(1, n, lambda i, c: (row(i, me).start(), c)[1], 0)
     keep.wait()
     xg.pass_on(z)
-    yg.across()
+
+    yg.across_early()
+
+    @pl.when(outer)
+    def _():
+        pg.first()
+        yg.first()
+        yg.across_late()
+
+    @pl.when(pg.inner)
+    def _():
+        pg.across()
+
     fetch.wait()
     turn = 16
     whole = width // turn * turn
@@ -452,7 +480,48 @@
             multiply(x_got[zz * CAPQ + r], zz * 2 + 1 - y, r)
         red.begin(zz)
 
+    quarter = nt // n_ga
+    weight = v_ref[...].reshape(1, width)
+    sets = jnp.where(pg.edged, 4, 2)
+    ered = Reduce(part3, eown, e1, et, e2, v1, w1, v2, w2, 4 * nz)
+
+    def of(q):
+        return jnp.where(q // 2 == 0, z, pg.edge) * 2 + q % 2
+
+    def joined(both, out, at):
+        v = jnp.concatenate(both, axis=1)
+        for i in range(n_ga):
+            out[i, at] = v[i * quarter : (i + 1) * quarter]
+
+    def exchange(q, carry):
+        a = of(q)
+        for k in range(per_dev):
+            weighted = p_all[a * per_dev + k].astype(F32) * weight
+            high = weighted.astype(BF16)
+            split[k, :nt] = high
+            split[k, nt:] = (weighted - high.astype(F32)).astype(BF16)
+
+        def level(zz, carry):
+            both = []
+            for r in range(CAPQ):
+                at = 3 * slots + (zz * 2 + y) * CAPQ + r
+                k2 = jnp.maximum(tab[a, at + slots], 0)
+                v = lax.dot_general(
+                    split[tab[a, at]], p_all[k2], DIMS, preferred_element_type=F32
+                )
+                both.append(v[:nt] + v[nt:])
+            joined(both, part3, q * nz + zz)
+            return carry
+
+        lax.fori_loop(0, nz, level, 0, unroll=2)
+        return carry
+
     xg.hop(1)
+
+    @pl.when(pg.inner)
+    def _():
+        pg.first()
+
     lax.fori_loop(
         1, n, lambda i, c: (row(i, lax.rem(me + n - i, n)).wait_recv(), c)[1], 0
     )
@@ -466,8 +535,12 @@
 
         @pl.when(h == 2)
         def _():
-            yg.first()
-            pg.first()
+            @pl.when(pg.inner)
+            def _():
+                lax.fori_loop(1, nz, lambda i, c: (pg.hop(i), c)[1], 0)
+                yg.first()
+
+            yg.second()
 
         @pl.when(h < nz)
         def _():
@@ -475,77 +548,50 @@
 
         @pl.when(h == 2)
         def _():
-            yg.second()
+            @pl.when(pg.inner)
+            def _():
+                pg.across_edge()
+                yg.across_late()
+
+            red.middle(z)
+
+        @pl.when(h > 2)
+        def _():
+            xg.sides(h - 2, lambda zz, way: red.middle(zz))
 
         xg.sides(h - 1, lambda zz, way: piece(zz))
 
-        @pl.when(h == 2)
-        def _():
-            red.middle(z)
-
-        @pl.when(h > 2)
-        def _():
-            xg.sides(h - 2, lambda zz, way: red.middle(zz))
-            yg.hop(h - 2)
-            pg.hop(h - 2)
+        @pl.when(h == 3)
+        def _():
+            pg.finish()
+
+        @pl.when(h > 3)
+        def _():
+            yg.hop(h - 3)
+
+        @pl.when(jnp.logical_and(jnp.logical_and(h >= 3, h <= 4), pg.inner))
+        def _():
+            low = (h - 3) * 2
+            lax.fori_loop(low, jnp.minimum(low + 2, sets), exchange, 0)
+
+            @pl.when(h == 4)
+            def _():
+                ered.begin(0)
 
         return carry
 
     lax.fori_loop(2, nz + 1, stage, 0)
     xg.sides(nz - 1, lambda zz, way: red.middle(zz))
-    yg.hop(nz - 1)
-    pg.hop(nz - 1)
-    xg.finish()
-    pg.finish()
-
-    quarter = nt // n_ga
-    weight = v_ref[...].reshape(1, width)
-    sets = jnp.where(pg.edged, 4, 2)
-    ered = Reduce(part3, eown, e1, et, e2, v1, w1, v2, w2, 4 * nz)
-
-    def of(q):
-        return jnp.where(q // 2 == 0, z, pg.edge) * 2 + q % 2
-
-    def joined(both, out, at):
-        v = jnp.concatenate(both, axis=1)
-        for i in range(n_ga):
-            out[i, at] = v[i * quarter : (i + 1) * quarter]
-
-    @pl.when(pg.inner)
-    def _():
-        def exchange(q, carry):
-            a = of(q)
-            for k in range(per_dev):
-                weighted = p_all[a * per_dev + k].astype(F32) * weight
-                high = weighted.astype(BF16)
-                split[k, :nt] = high
-                split[k, nt:] = (weighted - high.astype(F32)).astype(BF16)
-
-            def level(zz, carry):
-                both = []
-                for r in range(CAPQ):
-                    at = 3 * slots + (zz * 2 + y) * CAPQ + r
-                    k2 = jnp.maximum(tab[a, at + slots], 0)
-                    v = lax.dot_general(
-                        split[tab[a, at]], p_all[k2], DIMS, preferred_element_type=F32
-                    )
-                    both.append(v[:nt] + v[nt:])
-                joined(both, part3, q * nz + zz)
-                return carry
-
-            lax.fori_loop(0, nz, level, 0)
-            return carry
-
-        lax.fori_loop(0, sets, exchange, 0)
-        ered.begin(0)
-
-    lax.fori_loop(0, nz, lambda i, c: (red.end(i), c)[1], 0)
-    yg.finish()
+    yg.hop(nz - 2)
 
     @pl.when(pg.inner)
     def _():
         ered.middle(0)
 
+    yg.hop(nz - 1)
+    xg.finish()
+    lax.fori_loop(0, nz, lambda i, c: (red.end(i), c)[1], 0)
+    yg.finish()
     lax.fori_loop(1, n, lambda i, c: (row(i, me).wait_send(), c)[1], 0)
 
     def source(a, carry):

time: 71.3 us -> 65 us (0.912)
  Pallas kernels: 70.5 us -> 64.2 us
    pallas_call x1, Pallas kernels: 68.6 us -> 62.3 us  [per_device(): pl.pallas_call(functools.partial(kernel, n), out_shape=shape((n_ga, rows...]
where the time goes in v4:
time: 65 us; the launch traced here: 64.9 us
  Pallas kernels  64.2 us (99%)
    pallas_call x1, Pallas kernels, per_device(): pl.pallas_call(functools.partial(kernel, n), out_shape=shape((n_ga, rows...  62.3 us
    pallas_call x1, Pallas kernels, per_device(): pl.pallas_call(layout, out_shape=[shape((rows, nt * nt), F32), shape((per...  1.91 us

profile of v4, /device:TPU:0, one launch (start us, length us, event | category | flops | bytes accessed | tf_op | source)
XLA Modules:
  0.0 64.9 jit_solution(9841984948688430505)
XLA Ops:
  0.6 62.3 %window.1.lines = f32[4,160,128]{2,1,0:T(8,128)} custom-call(s32[3,16]{1,0:T(4,128)} %bitcast.3, s32[16]{0:T(128)} %qs_ref.1, bf16[4,64,375]{2,1,0:T(8,128)(2,1)} %x_ref.1, bf16[4,64,375]{2,1,0:T(8,128)(2,1)} %y_ref.1, bf16[4,64,375]{2,1,0:T(8,128)(2,1)} %p_ref.1, f32[375]{0:T(512)} %v_ref.1, bf16[375,2,1500]{2,1,0:T(2,128)(2,1)} %bitcast.2), custom_call_target="tpu_custom_call" | custom-call | tf_op jit(solution)/shard_map/window/pallas_call | solution.py:815
  62.9 1.9 %layout.1 = (f32[16,4096]{1,0:T(8,128)}, f32[4,4096]{1,0:T(4,128)}) custom-call(f32[4,160,128]{2,1,0:T(8,128)} %window.1.lines), custom_call_target="tpu_custom_call" | custom-call | tf_op jit(solution)/shard_map/layout/pallas_call | solution.py:872

commit v5 on v4

--- a/solution.py
+++ b/solution.py
@@ -70,10 +70,23 @@
         return remote(
             self.src.at[k] if own else block,
             block,
-            self.send.at[way * self.n * self.size + at],
+            self.send.at[way * self.n + zz * 2 + yy],
             self.recv.at[at],
             {"ka": target},
         )
+
+    def all_sent(self, zz, yy, way, count):
+        block = self.out.at[pl.ds((zz * 2 + yy) * self.size, count)]
+        done = self.send.at[way * self.n + zz * 2 + yy]
+        remote(block, block, done, done, {"ka": self.z * 2 + 1 - self.y}).wait_send()
+
+    def chained(self, zz, yy, count, ways=(0, 1)):
+        for way in ways:
+            free = self.z < self.nz - 1 if way == 0 else self.z > 0
+
+            @pl.when(free)
+            def _(way=way):
+                self.all_sent(zz, yy, way, count)
 
     def chain(self, zz, yy, k, act, ways=(0, 1), own=False):
         for way in ways:
@@ -130,22 +143,19 @@
             self.sides(h, lambda zz, way, k=k: one(k, 1 - self.y, zz, way))
 
     def finish(self):
-        for k in range(self.size):
-            self.chain(self.z, self.y, k, sent, own=True)
-            self.copy(self.z, self.y, k, 2, True).wait_send()
-        for k in self.early():
-            self.chain(self.z, 1 - self.y, k, sent)
+        few = len(self.early())
+        self.chained(self.z, self.y, self.size)
+        self.all_sent(self.z, self.y, 2, self.size)
+        self.chained(self.z, 1 - self.y, few)
         for k in range(self.cut):
             self.copy(self.z, 1 - self.y, k, 2).wait_recv()
 
         def tail(h, carry):
             def side(zz, way):
-                for k in range(self.size):
-                    self.chain(zz, self.y, k, sent, (way,))
-                for k in self.early():
-                    self.chain(zz, 1 - self.y, k, sent, (way,))
+                self.chained(zz, self.y, self.size, (way,))
+                self.chained(zz, 1 - self.y, few, (way,))
+                self.all_sent(zz, self.y, 2, self.cut)
                 for k in range(self.cut):
-                    self.copy(zz, self.y, k, 2).wait_send()
                     self.copy(zz, 1 - self.y, k, 2).wait_recv()
 
             self.sides(h, side)
@@ -161,6 +171,40 @@
         self.edged = jnp.logical_or(self.z == 1, self.z == self.nz - 2)
         self.edge = jnp.where(self.z == 1, 0, self.nz - 1)
 
+    def copy(self, zz, yy, k, way, own=False):
+        base = (zz * 2 + yy) * self.size
+        target = (self.z + (1 if way == 0 else -1)) * 2 + self.y
+        return remote(
+            self.src.at[k] if own else self.out.at[base + k],
+            self.out.at[base + k],
+            self.send.at[way * self.nz + zz],
+            self.recv.at[zz * self.size + k],
+            {"ka": target},
+        )
+
+    def cross(self, zz, yy, i):
+        block = self.out.at[pl.ds((zz * 2 + yy) * self.size, self.size)]
+        return remote(
+            self.src if i == 0 and yy is self.y else block,
+            block,
+            self.send.at[2 * self.nz + i],
+            self.recv.at[self.nz * self.size + i],
+            {"ka": self.z * 2 + 1 - self.y},
+        )
+
+    def all_sent(self, zz, yy, way, count):
+        block = self.out.at[pl.ds((zz * 2 + yy) * self.size, count)]
+        done = self.send.at[way * self.nz + zz]
+        remote(block, block, done, done, {"ka": self.z * 2 + 1 - self.y}).wait_send()
+
+    def chained(self, zz, yy, count, ways=(0, 1)):
+        for way in ways:
+            free = self.z <= self.nz - 3 if way == 0 else self.z >= 2
+
+            @pl.when(free)
+            def _(way=way):
+                self.all_sent(zz, yy, way, count)
+
     def chain(self, zz, yy, k, act, ways=(0, 1), own=False):
         for way in ways:
             free = self.z <= self.nz - 3 if way == 0 else self.z >= 2
@@ -175,8 +219,7 @@
         self.out[pl.ds(self.me * self.size, self.size)] = self.src[...]
 
     def across(self):
-        for k in range(self.size):
-            self.copy(self.z, self.y, k, 2, True).start()
+        self.cross(self.z, self.y, 0).start()
 
     def onward(self, zz, way):
         last = jnp.logical_and(self.edged, zz == self.edge)
@@ -190,7 +233,7 @@
             @pl.when(on)
             def _():
                 for k in range(self.size):
-                    self.copy(zz, self.y, k, 2).wait_recv()
+                    self.copy(zz, self.y, k, way).wait_recv()
                     self.chain(zz, self.y, k, start, (way,))
 
         self.sides(h, own)
@@ -198,34 +241,29 @@
     def across_edge(self):
         @pl.when(self.edged)
         def _():
-            for k in range(self.size):
-                self.copy(self.edge, self.y, k, 2).start()
+            self.cross(self.edge, self.y, 1).start()
 
     def finish(self):
-        for k in range(self.size):
-            self.chain(self.z, self.y, k, sent, own=True)
+        self.chained(self.z, self.y, self.size)
 
         @pl.when(self.inner)
         def _():
-            for k in range(self.size):
-                self.copy(self.z, self.y, k, 2, True).wait_send()
-                self.copy(self.z, 1 - self.y, k, 2).wait_recv()
+            self.cross(self.z, self.y, 0).wait_send()
+            self.cross(self.z, 1 - self.y, 0).wait_recv()
 
             @pl.when(self.edged)
             def _():
-                for k in range(self.size):
-                    self.copy(self.edge, self.y, k, 2).wait_send()
-                    self.copy(self.edge, 1 - self.y, k, 2).wait_recv()
+                self.cross(self.edge, self.y, 1).wait_send()
+                self.cross(self.edge, 1 - self.y, 1).wait_recv()
 
             def tail(h, carry):
                 def side(zz, way):
-                    on = self.onward(zz, way)
-                    for k in range(self.size):
-                        self.chain(zz, self.y, k, sent, (way,))
-
-                        @pl.when(jnp.logical_not(on))
-                        def _(k=k):
-                            self.copy(zz, self.y, k, 2).wait_recv()
+                    self.chained(zz, self.y, self.size, (way,))
+
+                    @pl.when(jnp.logical_not(self.onward(zz, way)))
+                    def _():
+                        for k in range(self.size):
+                            self.copy(zz, self.y, k, way).wait_recv()
 
                 self.sides(h, side)
                 return carry
@@ -248,7 +286,7 @@
         return remote(
             self.src.at[k] if own else self.col.at[at],
             self.col.at[at],
-            self.send.at[way * self.nz * self.size + at],
+            self.send.at[way * self.nz + zz],
             self.recv.at[at],
             {"ka": target},
         )
@@ -306,15 +344,23 @@
             self.out[zz * CAPQ + r] = self.chosen(zz, self.z * 2 + 1 - self.y, r)
         self.across(zz).start()
 
+    def chained(self, zz, ways=(0, 1)):
+        block = self.col.at[pl.ds(zz * self.size, self.size)]
+        for way in ways:
+            free = self.z < self.nz - 1 if way == 0 else self.z > 0
+            done = self.send.at[way * self.nz + zz]
+
+            @pl.when(free)
+            def _(done=done):
+                remote(block, block, done, done, {"ka": self.z * 2 + 1 - self.y}).wait_send()
+
     def finish(self):
-        for k in range(self.size):
-            self.chain(self.z, k, sent, own=True)
+        self.chained(self.z)
         self.across(self.z).wait_send()
 
         def tail(h, carry):
             def side(zz, way):
-                for k in range(self.size):
-                    self.chain(zz, k, sent, (way,))
+                self.chained(zz, (way,))
                 self.across(zz).wait_send()
 
             self.sides(h, side)
@@ -339,7 +385,7 @@
         return remote(
             self.part.at[xx * 2 + 1 - self.c, self.rows(i)],
             self.recv1.at[xx, self.rows(i)],
-            self.s1.at[i * 2 + t],
+            self.s1,
             self.r1.at[i * 2 + t],
             {"ga": self.x * 2 + 1 - self.c},
         )
@@ -348,7 +394,7 @@
         return remote(
             self.tsend.at[self.rows(i)],
             self.recv2.at[self.rows(i)],
-            self.s2.at[i],
+            self.s2,
             self.r2.at[i],
             {"ga": (1 - self.x) * 2 + self.c},
         )
@@ -372,9 +418,12 @@
         self.two(i).wait_recv()
         v = v + self.recv2[self.rows(i)].astype(F32)
         self.out[self.rows(i)] = v.astype(self.out.dtype)
-        self.one(0, i).wait_send()
-        self.one(1, i).wait_send()
-        self.two(i).wait_send()
+
+    def finish(self):
+        to = {"ga": self.x * 2 + 1 - self.c}
+        both = self.part.at[pl.ds(0, 2)]
+        remote(both, both, self.s1, self.s1, to).wait_send()
+        remote(self.tsend, self.tsend, self.s2, self.s2, to).wait_send()
 
 
 def make_row(n, q_slots, per_dev, pairs_ref, qs_ref, row_ref, at_ref):
@@ -406,10 +455,10 @@
 
 def kernel(n, pairs_ref, qs_ref, x_ref, y_ref, p_ref, v_ref, w_hbm, lines,
            tab, at_ref, row_ref, wt, w_ref, x_col, x_out, x_got, y_all, p_all, part, half,
-           recv1, tsend, recv2, part2, own, q1, qt, q2, second, outbox, inbox,
+           recv1, tsend, recv2, part2, own, q1, qt, q2, second, outbox, sumbox, inbox,
            split, part3, eown, e1, et, e2, ebox, ein, emir,
            ws, ls, ts, tr, xs, xr, xps, xpr, ys, yr, ps, pr, s1, r1, s2, r2, t1, u1, t2, u2,
-           v1, w1, v2, w2, es, er, fs, fr, as_, ar, gs, gr):
+           v1, w1, v2, w2, es, er, fs, fr, as_, ar, bs, br, gs, gr):
     per_dev, nt, width = x_ref.shape
     rows = pairs_ref.shape[1]
     q_slots = w_ref.shape[0]
@@ -561,38 +610,38 @@
 
         xg.sides(h - 1, lambda zz, way: piece(zz))
 
-        @pl.when(h == 3)
+        @pl.when(jnp.logical_and(h >= 3, h < nz))
         def _():
-            pg.finish()
-
-        @pl.when(h > 3)
-        def _():
-            yg.hop(h - 3)
-
-        @pl.when(jnp.logical_and(jnp.logical_and(h >= 3, h <= 4), pg.inner))
-        def _():
-            low = (h - 3) * 2
-            lax.fori_loop(low, jnp.minimum(low + 2, sets), exchange, 0)
-
-            @pl.when(h == 4)
-            def _():
-                ered.begin(0)
+            yg.hop(h - 2)
 
         return carry
 
     lax.fori_loop(2, nz + 1, stage, 0)
+    pg.finish()
+
+    @pl.when(pg.inner)
+    def _():
+        lax.fori_loop(0, 2, exchange, 0)
+
     xg.sides(nz - 1, lambda zz, way: red.middle(zz))
     yg.hop(nz - 2)
+
+    @pl.when(pg.inner)
+    def _():
+        lax.fori_loop(2, sets, exchange, 0)
+        ered.begin(0)
+
+    yg.hop(nz - 1)
 
     @pl.when(pg.inner)
     def _():
         ered.middle(0)
 
-    yg.hop(nz - 1)
     xg.finish()
     lax.fori_loop(0, nz, lambda i, c: (red.end(i), c)[1], 0)
     yg.finish()
     lax.fori_loop(1, n, lambda i, c: (row(i, me).wait_send(), c)[1], 0)
+    red.finish()
 
     def source(a, carry):
         both = []
@@ -604,9 +653,10 @@
         joined(both, part2, a)
         return carry
 
-    lax.fori_loop(0, n, source, 0, unroll=2)
-    end = Reduce(part2, own, q1, qt, q2, t1, u1, t2, u2, n)
-    end.begin(0)
+    end = Reduce(part2, own, q1, qt, q2, t1, u1, t2, u2, n // 2)
+    for i in range(2):
+        lax.fori_loop(i * n // 2, (i + 1) * n // 2, source, 0, unroll=2)
+        end.begin(i)
     shape = own.shape[1:]
     left = lax.broadcasted_iota(I32, shape, 1) < nt
     doubles = per_dev // 2
@@ -630,7 +680,7 @@
         )
 
     def to_second(zz):
-        return remote(ebox.at[zz], emir.at[z], fs.at[zz], fr.at[z], {"ka": zz * 2 + y})
+        return remote(ebox.at[zz], emir.at[z], fs, fr.at[z], {"ka": zz * 2 + y})
 
     def others(act):
         def one(q, carry):
@@ -655,6 +705,7 @@
     @pl.when(pg.inner)
     def _():
         ered.end(0)
+        ered.finish()
         others(start)
         ein[y] = eown[pl.ds(y * nz, nz)]
 
@@ -680,10 +731,20 @@
         emir[z] = ebox[z]
 
     end.middle(0)
+    end.middle(1)
+
+    def cross(src, box, i, whose, ss, rs):
+        to = lax.rem(me + i, n)
+        return remote(src.at[to], box.at[whose], ss, rs.at[whose], {"ka": to})
+
     end.end(0)
-
-    def fill(b, carry):
-        outbox[b, 0] = own[b]
+    end.end(1)
+    end.finish()
+    lax.fori_loop(1, n, lambda i, c: (cross(own, inbox, i, me, as_, ar).start(), c)[1], 0)
+    inbox[me] = own[me]
+
+    def fill(i, carry):
+        b = lax.rem(me + i, n)
 
         def add(a, sums):
             out = []
@@ -693,18 +754,18 @@
 
         sums = tuple(jnp.zeros(shape, F32) for _ in range(per_dev))
         sums = lax.fori_loop(0, n, add, sums, unroll=min(n, 8))
-        for i, v in enumerate(paired(sums)):
-            outbox[b, 1 + i] = v
+        for i_, v in enumerate(paired(sums)):
+            outbox[b, i_] = v
+
+        @pl.when(i > 0)
+        def _():
+            cross(outbox, sumbox, i, me, bs, br).start()
+
         return carry
 
-    lax.fori_loop(0, n, fill, 0)
-
-    def cross(i, whose):
-        to = lax.rem(me + i, n)
-        return remote(outbox.at[to], inbox.at[whose], as_.at[i], ar.at[whose], {"ka": to})
-
-    lax.fori_loop(1, n, lambda i, c: (cross(i, me).start(), c)[1], 0)
-    inbox[me] = outbox[me]
+    lax.fori_loop(1, n, fill, 0)
+    fill(jnp.int32(0), 0)
+    sumbox[me] = outbox[me]
     for yy in range(2):
 
         @pl.when(jnp.logical_or(jnp.logical_not(pg.inner), yy != y))
@@ -715,19 +776,27 @@
         @pl.when(zz != z)
         def _():
             remote(
-                emir.at[zz], emir.at[zz], fs.at[0], fr.at[zz], {"ka": z * 2 + 1 - y}
+                emir.at[zz], emir.at[zz], fs, fr.at[zz], {"ka": z * 2 + 1 - y}
             ).wait_recv()
 
         return carry
 
     lax.fori_loop(1, nz - 1, inner_level, 0)
-    lax.fori_loop(1, n, lambda i, c: (cross(i, lax.rem(me + n - i, n)).wait_recv(), c)[1], 0)
-    lax.fori_loop(1, n, lambda i, c: (cross(i, me).wait_send(), c)[1], 0)
+    for box, src, ss, rs in ((inbox, own, as_, ar), (sumbox, outbox, bs, br)):
+
+        def arrived(i, carry, box=box, src=src, ss=ss, rs=rs):
+            cross(src, box, i, lax.rem(me + n - i, n), ss, rs).wait_recv()
+            return carry
+
+        lax.fori_loop(1, n, arrived, 0)
+        rest = src.at[pl.ds(0, n - 1)]
+        remote(rest, rest, ss, ss, {"ka": z * 2 + 1 - y}).wait_send()
 
     @pl.when(pg.inner)
     def _():
         others(sent)
-        levels(sent)
+        rest = ebox.at[pl.ds(0, nz - 1)]
+        remote(rest, rest, fs, fs, {"ka": z * 2 + 1 - y}).wait_send()
 
     sub = quarter // 2
 
@@ -741,13 +810,13 @@
     for j in range(rows):
         at, et_ = at_ref[0, j], at_ref[1, j]
         b = et_ // CAPQ
-        direct = picked(inbox, (at // CAPQ, 0), at % CAPQ)
+        direct = picked(inbox, (at // CAPQ,), at % CAPQ)
         term = picked(ein, (b % 2, b // 2), et_ % CAPQ)
         lines[g, pl.ds(j * sub, sub)] = 2.0 * term - direct
     base = rows * sub
     for i in range(doubles):
         total = lax.fori_loop(
-            1, n, lambda o, t, i=i: t + inbox[o, 1 + i], inbox[0, 1 + i]
+            1, n, lambda o, t, i=i: t + sumbox[o, i], sumbox[0, i]
         )
         term = lax.fori_loop(
             2, nz - 1, lambda zz, t, i=i: t + emir[zz, i], emir[1, i]
@@ -810,6 +879,7 @@
     each = (quarter, CAPQ * nt)
     line = (n,) + each
     dma = lambda m: pltpu.SemaphoreType.DMA((m,))
+    one = pltpu.SemaphoreType.DMA
     row_len = -(-5 * slots // 128) * 128
     k_all = n * per_dev
     lines = pl.pallas_call(
@@ -839,8 +909,9 @@
             pltpu.VMEM(line, F32),
             pltpu.VMEM(line, F32),
             pltpu.VMEM(line, I32),
-            pltpu.VMEM((n, 1 + per_dev // 2) + each, F32),
-            pltpu.VMEM((n, 1 + per_dev // 2) + each, F32),
+            pltpu.VMEM((n, per_dev // 2) + each, F32),
+            pltpu.VMEM((n, per_dev // 2) + each, F32),
+            pltpu.VMEM(line, F32),
             pltpu.VMEM((per_dev, 2 * nt, g), BF16),
             pltpu.VMEM((n_ga, 4 * nz) + each, F32),
             pltpu.VMEM((4 * nz,) + each, F32),
@@ -850,18 +921,17 @@
             pltpu.VMEM((nz, per_dev // 2) + each, F32),
             pltpu.VMEM((2, nz) + each, F32),
             pltpu.VMEM((nz, per_dev // 2) + each, F32),
-            pltpu.SemaphoreType.DMA,
-            pltpu.SemaphoreType.DMA,
+            one, one,
             dma(n), dma(n),
-            dma(2 * nz * per_dev), dma(nz * per_dev),
+            dma(2 * nz), dma(nz * per_dev),
             dma(nz), dma(nz),
-            dma(3 * k_all), dma(k_all),
-            dma(3 * k_all), dma(k_all),
-            dma(2 * nz), dma(2 * nz), dma(nz), dma(nz),
-            dma(2), dma(2), dma(1), dma(1),
-            dma(2), dma(2), dma(1), dma(1),
-            dma(4), dma(2), dma(nz), dma(nz),
-            dma(n), dma(n),
+            dma(3 * n), dma(k_all),
+            dma(2 * nz + 2), dma(nz * per_dev + 2),
+            one, dma(2 * nz), one, dma(nz),
+            one, dma(4), one, dma(2),
+            one, dma(2), one, dma(1),
+            dma(4), dma(2), one, dma(nz),
+            one, dma(n), one, dma(n),
             dma(3), dma(3),
         ],
         compiler_params=pltpu.CompilerParams(

time: 65 us -> 62.9 us (0.968)
  Pallas kernels: 64.2 us -> 62.1 us
    pallas_call x1, Pallas kernels: 62.3 us -> 60.2 us  [per_device(): pl.pallas_call(functools.partial(kernel, n), out_shape=shape((n_ga, rows...]
where the time goes in v5:
time: 62.9 us; the launch traced here: 62.7 us
  Pallas kernels  62.1 us (99%)
  between operations  0.64 us (1%)
    pallas_call x1, Pallas kernels, per_device(): pl.pallas_call(functools.partial(kernel, n), out_shape=shape((n_ga, rows...  60.2 us
    pallas_call x1, Pallas kernels, per_device(): pl.pallas_call(layout, out_shape=[shape((rows, nt * nt), F32), shape((per...  1.91 us

profile of v5, /device:TPU:0, one launch (start us, length us, event | category | flops | bytes accessed | tf_op | source)
XLA Modules:
  0.0 62.7 jit_solution(11655186671861423208)
XLA Ops:
  0.6 60.2 %window.1.lines = f32[4,160,128]{2,1,0:T(8,128)} custom-call(s32[3,16]{1,0:T(4,128)} %bitcast.3, s32[16]{0:T(128)} %qs_ref.1, bf16[4,64,375]{2,1,0:T(8,128)(2,1)} %x_ref.1, bf16[4,64,375]{2,1,0:T(8,128)(2,1)} %y_ref.1, bf16[4,64,375]{2,1,0:T(8,128)(2,1)} %p_ref.1, f32[375]{0:T(512)} %v_ref.1, bf16[375,2,1500]{2,1,0:T(2,128)(2,1)} %bitcast.2), custom_call_target="tpu_custom_call" | custom-call | tf_op jit(solution)/shard_map/window/pallas_call | solution.py:885
  60.8 1.9 %layout.1 = (f32[16,4096]{1,0:T(8,128)}, f32[4,4096]{1,0:T(4,128)}) custom-call(f32[4,160,128]{2,1,0:T(8,128)} %window.1.lines), custom_call_target="tpu_custom_call" | custom-call | tf_op jit(solution)/shard_map/layout/pallas_call | solution.py:942

commit v6 on v5

--- a/solution.py
+++ b/solution.py
@@ -126,12 +126,12 @@
             def _(zz=zz, way=way):
                 act(zz, way)
 
-    def hop(self, h):
+    def hop(self, h, low=0, high=None):
         def one(k, yy, zz, way):
             self.copy(zz, yy, k, 2).wait_recv()
             self.chain(zz, yy, k, start, (way,))
 
-        for k in range(self.size):
+        for k in range(self.size)[low:high]:
 
             def own(zz, way, k=k):
                 one(k, self.y, zz, way)
@@ -139,7 +139,7 @@
                     self.copy(zz, self.y, k, 2).start()
 
             self.sides(h, own)
-        for k in self.early():
+        for k in self.early() if high is None else ():
             self.sides(h, lambda zz, way, k=k: one(k, 1 - self.y, zz, way))
 
     def finish(self):
@@ -221,51 +221,50 @@
     def across(self):
         self.cross(self.z, self.y, 0).start()
 
-    def onward(self, zz, way):
-        last = jnp.logical_and(self.edged, zz == self.edge)
-        free = self.z <= self.nz - 3 if way == 0 else self.z >= 2
-        return jnp.logical_or(last, free)
-
     def hop(self, h):
         def own(zz, way):
-            on = self.onward(zz, way)
-
-            @pl.when(on)
-            def _():
-                for k in range(self.size):
+            end = jnp.logical_and(self.edged, zz == self.edge)
+            for k in range(self.size):
+
+                @pl.when(jnp.logical_not(end))
+                def _(k=k):
                     self.copy(zz, self.y, k, way).wait_recv()
-                    self.chain(zz, self.y, k, start, (way,))
+
+                self.chain(zz, self.y, k, start, (way,))
 
         self.sides(h, own)
+
+    def crossed(self):
+        self.cross(self.z, 1 - self.y, 0).wait_recv()
+
+        @pl.when(self.edged)
+        def _():
+            self.cross(self.edge, 1 - self.y, 1).wait_recv()
 
     def across_edge(self):
         @pl.when(self.edged)
         def _():
             self.cross(self.edge, self.y, 1).start()
 
+    def edge_in(self):
+        @pl.when(self.edged)
+        def _():
+            for k in range(self.size):
+                self.copy(self.edge, self.y, k, 2).wait_recv()
+
     def finish(self):
         self.chained(self.z, self.y, self.size)
 
         @pl.when(self.inner)
         def _():
             self.cross(self.z, self.y, 0).wait_send()
-            self.cross(self.z, 1 - self.y, 0).wait_recv()
 
             @pl.when(self.edged)
             def _():
                 self.cross(self.edge, self.y, 1).wait_send()
-                self.cross(self.edge, 1 - self.y, 1).wait_recv()
 
             def tail(h, carry):
-                def side(zz, way):
-                    self.chained(zz, self.y, self.size, (way,))
-
-                    @pl.when(jnp.logical_not(self.onward(zz, way)))
-                    def _():
-                        for k in range(self.size):
-                            self.copy(zz, self.y, k, way).wait_recv()
-
-                self.sides(h, side)
+                self.sides(h, lambda zz, way: self.chained(zz, self.y, self.size, (way,)))
                 return carry
 
             lax.fori_loop(1, self.nz, tail, 0)
@@ -416,8 +415,11 @@
         self.one(1, i).wait_recv()
         v = self.sum_one(self.x, i)
         self.two(i).wait_recv()
-        v = v + self.recv2[self.rows(i)].astype(F32)
-        self.out[self.rows(i)] = v.astype(self.out.dtype)
+        v = (v + self.recv2[self.rows(i)].astype(F32)).astype(self.out.dtype)
+        if len(self.out.shape) == len(self.tsend.shape):
+            self.out[self.rows(i)] = v
+        else:
+            self.out[i] = v
 
     def finish(self):
         to = {"ga": self.x * 2 + 1 - self.c}
@@ -532,7 +534,7 @@
     quarter = nt // n_ga
     weight = v_ref[...].reshape(1, width)
     sets = jnp.where(pg.edged, 4, 2)
-    ered = Reduce(part3, eown, e1, et, e2, v1, w1, v2, w2, 4 * nz)
+    ered = Reduce(part3, eown, e1, et, e2, v1, w1, v2, w2, 4)
 
     def of(q):
         return jnp.where(q // 2 == 0, z, pg.edge) * 2 + q % 2
@@ -542,28 +544,35 @@
         for i in range(n_ga):
             out[i, at] = v[i * quarter : (i + 1) * quarter]
 
-    def exchange(q, carry):
-        a = of(q)
+    def weigh(q, carry):
         for k in range(per_dev):
-            weighted = p_all[a * per_dev + k].astype(F32) * weight
+            weighted = p_all[of(q) * per_dev + k].astype(F32) * weight
             high = weighted.astype(BF16)
-            split[k, :nt] = high
-            split[k, nt:] = (weighted - high.astype(F32)).astype(BF16)
-
-        def level(zz, carry):
+            split[q * per_dev + k, :nt] = high
+            split[q * per_dev + k, nt:] = (weighted - high.astype(F32)).astype(BF16)
+        return carry
+
+    def exchange(zz):
+        base = (zz * 2 + y) * per_dev
+
+        def one(q, carry):
+            a = of(q)
             both = []
             for r in range(CAPQ):
                 at = 3 * slots + (zz * 2 + y) * CAPQ + r
-                k2 = jnp.maximum(tab[a, at + slots], 0)
+                which = tab[a, at + slots] - base
+                other = p_all[base]
+                for k in range(1, per_dev):
+                    other = jnp.where(which == k, p_all[base + k], other)
                 v = lax.dot_general(
-                    split[tab[a, at]], p_all[k2], DIMS, preferred_element_type=F32
+                    split[q * per_dev + tab[a, at]], other, DIMS, preferred_element_type=F32
                 )
                 both.append(v[:nt] + v[nt:])
-            joined(both, part3, q * nz + zz)
+            joined(both, part3, zz * 4 + q)
             return carry
 
-        lax.fori_loop(0, nz, level, 0, unroll=2)
-        return carry
+        lax.fori_loop(0, sets, one, 0)
+        ered.begin(zz)
 
     xg.hop(1)
 
@@ -586,7 +595,6 @@
         def _():
             @pl.when(pg.inner)
             def _():
-                lax.fori_loop(1, nz, lambda i, c: (pg.hop(i), c)[1], 0)
                 yg.first()
 
             yg.second()
@@ -599,6 +607,7 @@
         def _():
             @pl.when(pg.inner)
             def _():
+                pg.edge_in()
                 pg.across_edge()
                 yg.across_late()
 
@@ -617,25 +626,48 @@
         return carry
 
     lax.fori_loop(2, nz + 1, stage, 0)
-    pg.finish()
 
     @pl.when(pg.inner)
     def _():
-        lax.fori_loop(0, 2, exchange, 0)
+        pg.hop(1)
+        pg.crossed()
+        lax.fori_loop(0, sets, weigh, 0)
+        exchange(z)
 
     xg.sides(nz - 1, lambda zz, way: red.middle(zz))
-    yg.hop(nz - 2)
+    half_way = per_dev // 2
+    yg.hop(nz - 2, 0, half_way)
 
     @pl.when(pg.inner)
     def _():
-        lax.fori_loop(2, sets, exchange, 0)
-        ered.begin(0)
-
-    yg.hop(nz - 1)
+        pg.sides(1, lambda zz, way: exchange(zz))
+
+    yg.hop(nz - 2, half_way)
 
     @pl.when(pg.inner)
     def _():
-        ered.middle(0)
+        ered.middle(z)
+        pg.sides(1, lambda zz, way: ered.middle(zz))
+
+    @pl.when(pg.inner)
+    def _():
+        def level(h, carry):
+            pg.hop(h)
+            pg.sides(h, lambda zz, way: exchange(zz))
+            return carry
+
+        lax.fori_loop(2, nz, level, 0)
+
+    pg.finish()
+    yg.hop(nz - 1)
+
+    @pl.when(pg.inner)
+    def _():
+        def level(h, carry):
+            pg.sides(h, lambda zz, way: ered.middle(zz))
+            return carry
+
+        lax.fori_loop(2, nz, level, 0)
 
     xg.finish()
     lax.fori_loop(0, nz, lambda i, c: (red.end(i), c)[1], 0)
@@ -676,7 +708,7 @@
 
     def to_first(q):
         return remote(
-            eown.at[pl.ds(q * nz, nz)], ein.at[y], es.at[q], er.at[y], {"ka": of(q)}
+            eown.at[:, q], ein.at[y], es.at[q], er.at[y], {"ka": of(q)}
         )
 
     def to_second(zz):
@@ -702,18 +734,21 @@
 
         lax.fori_loop(0, nz, one, 0)
 
+    end.middle(0)
+    end.middle(1)
+
     @pl.when(pg.inner)
     def _():
-        ered.end(0)
+        lax.fori_loop(0, nz, lambda i, c: (ered.end(i), c)[1], 0)
         ered.finish()
         others(start)
-        ein[y] = eown[pl.ds(y * nz, nz)]
+        ein[y] = eown[:, y]
 
         def level(zz, carry):
             def add(q, sums):
                 at = 4 * slots + (zz * 2 + y) * CAPQ
                 k2 = jnp.where(left, tab[of(q), at], tab[of(q), at + 1])
-                v = eown[q * nz + zz]
+                v = eown[zz, q]
                 base = (zz * 2 + y) * per_dev
                 return tuple(
                     t + jnp.where(k2 == base + i, v, 0.0) for i, t in enumerate(sums)
@@ -730,9 +765,6 @@
         levels(start)
         emir[z] = ebox[z]
 
-    end.middle(0)
-    end.middle(1)
-
     def cross(src, box, i, whose, ss, rs):
         to = lax.rem(me + i, n)
         return remote(src.at[to], box.at[whose], ss, rs.at[whose], {"ka": to})
@@ -782,22 +814,14 @@
         return carry
 
     lax.fori_loop(1, nz - 1, inner_level, 0)
-    for box, src, ss, rs in ((inbox, own, as_, ar), (sumbox, outbox, bs, br)):
-
-        def arrived(i, carry, box=box, src=src, ss=ss, rs=rs):
+    def arrived(box, src, ss, rs):
+        def one(i, carry):
             cross(src, box, i, lax.rem(me + n - i, n), ss, rs).wait_recv()
             return carry
 
-        lax.fori_loop(1, n, arrived, 0)
-        rest = src.at[pl.ds(0, n - 1)]
-        remote(rest, rest, ss, ss, {"ka": z * 2 + 1 - y}).wait_send()
-
-    @pl.when(pg.inner)
-    def _():
-        others(sent)
-        rest = ebox.at[pl.ds(0, nz - 1)]
-        remote(rest, rest, fs, fs, {"ka": z * 2 + 1 - y}).wait_send()
-
+        lax.fori_loop(1, n, one, 0)
+
+    arrived(inbox, own, as_, ar)
     sub = quarter // 2
 
     def picked(ref, at, r):
@@ -814,6 +838,17 @@
         term = picked(ein, (b % 2, b // 2), et_ % CAPQ)
         lines[g, pl.ds(j * sub, sub)] = 2.0 * term - direct
     base = rows * sub
+    x, c = g // 2, g % 2
+    mate, far = x * 2 + 1 - c, (1 - x) * 2 + c
+    parts = (pl.ds(0, base), pl.ds(base, doubles * quarter))
+
+    def spread(i, m, whose, to):
+        block = lines.at[whose, parts[m]]
+        return remote(block, block, gs.at[i * 2 + m], gr.at[i * 2 + m], {"ga": to})
+
+    spread(0, 0, g, far).start()
+    spread(1, 0, g, mate).start()
+    arrived(sumbox, outbox, bs, br)
     for i in range(doubles):
         total = lax.fori_loop(
             1, n, lambda o, t, i=i: t + sumbox[o, i], sumbox[0, i]
@@ -822,21 +857,26 @@
             2, nz - 1, lambda zz, t, i=i: t + emir[zz, i], emir[1, i]
         )
         lines[g, pl.ds(base + i * quarter, quarter)] = 2.0 * term - total
-    x, c = g // 2, g % 2
-    mate, far = x * 2 + 1 - c, (1 - x) * 2 + c
-
-    def spread(i, whose, to):
-        return remote(lines.at[whose], lines.at[whose], gs.at[i], gr.at[i], {"ga": to})
-
-    spread(0, g, far).start()
-    spread(1, g, mate).start()
-    spread(0, far, far).wait_recv()
-    spread(2, far, mate).start()
-    spread(1, mate, mate).wait_recv()
-    spread(2, (1 - x) * 2 + 1 - c, mate).wait_recv()
-    spread(0, g, far).wait_send()
-    spread(1, g, mate).wait_send()
-    spread(2, far, mate).wait_send()
+    spread(0, 1, g, far).start()
+    spread(1, 1, g, mate).start()
+    for m in range(2):
+        spread(0, m, far, far).wait_recv()
+        spread(2, m, far, mate).start()
+    for src, ss in ((own, as_), (outbox, bs)):
+        rest = src.at[pl.ds(0, n - 1)]
+        remote(rest, rest, ss, ss, {"ka": z * 2 + 1 - y}).wait_send()
+    @pl.when(pg.inner)
+    def _():
+        others(sent)
+        rest = ebox.at[pl.ds(0, nz - 1)]
+        remote(rest, rest, fs, fs, {"ka": z * 2 + 1 - y}).wait_send()
+
+    for m in range(2):
+        spread(1, m, mate, mate).wait_recv()
+        spread(2, m, (1 - x) * 2 + 1 - c, mate).wait_recv()
+        spread(0, m, g, far).wait_send()
+        spread(1, m, g, mate).wait_send()
+        spread(2, m, far, mate).wait_send()
 
 
 def layout(lines, blocks_ref, mirr_ref, turned, flat):
@@ -912,9 +952,9 @@
             pltpu.VMEM((n, per_dev // 2) + each, F32),
             pltpu.VMEM((n, per_dev // 2) + each, F32),
             pltpu.VMEM(line, F32),
-            pltpu.VMEM((per_dev, 2 * nt, g), BF16),
+            pltpu.VMEM((4 * per_dev, 2 * nt, g), BF16),
             pltpu.VMEM((n_ga, 4 * nz) + each, F32),
-            pltpu.VMEM((4 * nz,) + each, F32),
+            pltpu.VMEM((nz, 4) + each, F32),
             pltpu.VMEM((2, 4 * nz) + each, F32),
             pltpu.VMEM((4 * nz,) + each, F32),
             pltpu.VMEM((4 * nz,) + each, F32),
@@ -929,10 +969,10 @@
             dma(2 * nz + 2), dma(nz * per_dev + 2),
             one, dma(2 * nz), one, dma(nz),
             one, dma(4), one, dma(2),
-            one, dma(2), one, dma(1),
+            one, dma(2 * nz), one, dma(nz),
             dma(4), dma(2), one, dma(nz),
             one, dma(n), one, dma(n),
-            dma(3), dma(3),
+            dma(6), dma(6),
         ],
         compiler_params=pltpu.CompilerParams(
             collective_id=0, has_side_effects=True, vmem_limit_bytes=LIMIT

time: 62.9 us -> 59.6 us (0.948)
  Pallas kernels: 62.1 us -> 58.8 us
    pallas_call x1, Pallas kernels: 60.2 us -> 56.9 us  [per_device(): pl.pallas_call(functools.partial(kernel, n), out_shape=shape((n_ga, rows...]
where the time goes in v6:
time: 59.6 us; the launch traced here: 59.4 us
  Pallas kernels  58.8 us (99%)
  between operations  0.64 us (1%)
    pallas_call x1, Pallas kernels, per_device(): pl.pallas_call(functools.partial(kernel, n), out_shape=shape((n_ga, rows...  56.9 us
    pallas_call x1, Pallas kernels, per_device(): pl.pallas_call(layout, out_shape=[shape((rows, nt * nt), F32), shape((per...  1.91 us

profile of v6, /device:TPU:0, one launch (start us, length us, event | category | flops | bytes accessed | tf_op | source)
XLA Modules:
  0.0 59.4 jit_solution(3999056695015991917)
XLA Ops:
  0.6 56.9 %window.1.lines = f32[4,160,128]{2,1,0:T(8,128)} custom-call(s32[3,16]{1,0:T(4,128)} %bitcast.3, s32[16]{0:T(128)} %qs_ref.1, bf16[4,64,375]{2,1,0:T(8,128)(2,1)} %x_ref.1, bf16[4,64,375]{2,1,0:T(8,128)(2,1)} %y_ref.1, bf16[4,64,375]{2,1,0:T(8,128)(2,1)} %p_ref.1, f32[375]{0:T(512)} %v_ref.1, bf16[375,2,1500]{2,1,0:T(2,128)(2,1)} %bitcast.2), custom_call_target="tpu_custom_call" | custom-call | tf_op jit(solution)/shard_map/window/pallas_call | solution.py:925
  57.5 1.9 %layout.1 = (f32[16,4096]{1,0:T(8,128)}, f32[4,4096]{1,0:T(4,128)}) custom-call(f32[4,160,128]{2,1,0:T(8,128)} %window.1.lines), custom_call_target="tpu_custom_call" | custom-call | tf_op jit(solution)/shard_map/layout/pallas_call | solution.py:982

commit v7 on v6

--- a/solution.py
+++ b/solution.py
@@ -36,19 +36,29 @@
     )
 
 
-def greet(n):
+def greet(n, meanwhile):
     barrier = pltpu.get_barrier_semaphore()
     me = lax.axis_index("ka")
     g = lax.axis_index("ga")
-    n_ga = lax.axis_size("ga")
+    z, y = me // 2, me % 2
+    nz = n // 2
 
     def hello(to):
         pl.semaphore_signal(barrier, inc=1, device_id=to, device_id_type=pl.DeviceIdType.MESH)
 
-    lax.fori_loop(1, n, lambda i, c: (hello({"ka": lax.rem(me + i, n)}), c)[1], 0)
-    for i in range(1, n_ga):
-        hello({"ga": lax.rem(g + i, n_ga)})
-    pl.semaphore_wait(barrier, n - 1 + n_ga - 1)
+    @pl.when(z > 0)
+    def _():
+        hello({"ka": me - 2})
+
+    @pl.when(z < nz - 1)
+    def _():
+        hello({"ka": me + 2})
+
+    hello({"ka": z * 2 + 1 - y})
+    hello({"ga": g // 2 * 2 + 1 - g % 2})
+    hello({"ga": (1 - g // 2) * 2 + g % 2})
+    meanwhile()
+    pl.semaphore_wait(barrier, 5 - jnp.where(z > 0, 0, 1) - jnp.where(z < nz - 1, 0, 1))
 
 
 class Gather:
@@ -157,6 +167,34 @@
                 self.all_sent(zz, self.y, 2, self.cut)
                 for k in range(self.cut):
                     self.copy(zz, 1 - self.y, k, 2).wait_recv()
+
+            self.sides(h, side)
+            return carry
+
+        lax.fori_loop(1, self.nz, tail, 0)
+
+
+class Rows(Gather):
+    def all_sent(self, zz, yy, way, count):
+        block = self.out.at[zz * 2 + yy]
+        done = self.send.at[way * self.n + zz * 2 + yy]
+        remote(block, block, done, done, {"ka": self.z * 2 + 1 - self.y}).wait_send()
+
+    def begin(self):
+        self.chain(self.z, self.y, 0, start, own=True)
+        self.copy(self.z, self.y, 0, 2, True).start()
+
+    def other(self, zz):
+        self.copy(zz, 1 - self.y, 0, 2).wait_recv()
+
+    def finish(self):
+        self.chained(self.z, self.y, 1)
+        self.all_sent(self.z, self.y, 2, 1)
+
+        def tail(h, carry):
+            def side(zz, way):
+                self.chained(zz, self.y, 1, (way,))
+                self.all_sent(zz, self.y, 2, 1)
 
             self.sides(h, side)
             return carry
@@ -472,22 +510,17 @@
     z, y = me // 2, me % 2
     fetch = pltpu.make_async_copy(w_hbm, wt, ws)
     fetch.start()
-    greet(n)
+    greet(n, lambda: make_row(n, q_slots, per_dev, pairs_ref, qs_ref, row_ref, at_ref))
     xg = Pick(n, x_ref, x_col, x_out, x_got, tab, xs, xr, xps, xpr)
     yg = Gather(n, y_ref, y_all, ys, yr, per_dev - 1)
     pg = Hub(n, p_ref, p_all, ps, pr)
     outer = jnp.logical_not(pg.inner)
+    keep = pltpu.make_async_copy(row_ref.at[0], tab.at[me], ls)
+
+    rg = Rows(n, row_ref, tab, ts, tr, 1)
+    rg.begin()
     xg.first()
-    make_row(n, q_slots, per_dev, pairs_ref, qs_ref, row_ref, at_ref)
-    keep = pltpu.make_async_copy(row_ref.at[0], tab.at[me], ls)
     keep.start()
-
-    def row(i, whose):
-        return remote(
-            row_ref.at[0], tab.at[whose], ts.at[i], tr.at[whose], {"ka": lax.rem(me + i, n)}
-        )
-
-    lax.fori_loop(1, n, lambda i, c: (row(i, me).start(), c)[1], 0)
     keep.wait()
     xg.pass_on(z)
 
@@ -526,6 +559,7 @@
     def piece(zz):
         for r in range(CAPQ):
             multiply(xg.chosen(zz, me, r), zz * 2 + y, r)
+        rg.other(zz)
         xg.across(zz).wait_recv()
         for r in range(CAPQ):
             multiply(x_got[zz * CAPQ + r], zz * 2 + 1 - y, r)
@@ -574,21 +608,20 @@
         lax.fori_loop(0, sets, one, 0)
         ered.begin(zz)
 
+    rg.hop(1)
     xg.hop(1)
 
     @pl.when(pg.inner)
     def _():
         pg.first()
 
-    lax.fori_loop(
-        1, n, lambda i, c: (row(i, lax.rem(me + n - i, n)).wait_recv(), c)[1], 0
-    )
     xg.sides(1, lambda zz, way: xg.pass_on(zz))
     piece(z)
 
     def stage(h, carry):
         @pl.when(h < nz)
         def _():
+            rg.hop(h)
             xg.hop(h)
 
         @pl.when(h == 2)
@@ -672,7 +705,7 @@
     xg.finish()
     lax.fori_loop(0, nz, lambda i, c: (red.end(i), c)[1], 0)
     yg.finish()
-    lax.fori_loop(1, n, lambda i, c: (row(i, me).wait_send(), c)[1], 0)
+    rg.finish()
     red.finish()
 
     def source(a, carry):
@@ -767,7 +800,7 @@
 
     def cross(src, box, i, whose, ss, rs):
         to = lax.rem(me + i, n)
-        return remote(src.at[to], box.at[whose], ss, rs.at[whose], {"ka": to})
+        return remote(src.at[to], box.at[whose], ss, rs, {"ka": to})
 
     end.end(0)
     end.end(1)
@@ -814,14 +847,11 @@
         return carry
 
     lax.fori_loop(1, nz - 1, inner_level, 0)
-    def arrived(box, src, ss, rs):
-        def one(i, carry):
-            cross(src, box, i, lax.rem(me + n - i, n), ss, rs).wait_recv()
-            return carry
-
-        lax.fori_loop(1, n, one, 0)
-
-    arrived(inbox, own, as_, ar)
+    def arrived(box, rs):
+        rest = box.at[pl.ds(0, n - 1)]
+        remote(rest, rest, rs, rs, {"ka": z * 2 + 1 - y}).wait_recv()
+
+    arrived(inbox, ar)
     sub = quarter // 2
 
     def picked(ref, at, r):
@@ -848,7 +878,7 @@
 
     spread(0, 0, g, far).start()
     spread(1, 0, g, mate).start()
-    arrived(sumbox, outbox, bs, br)
+    arrived(sumbox, br)
     for i in range(doubles):
         total = lax.fori_loop(
             1, n, lambda o, t, i=i: t + sumbox[o, i], sumbox[0, i]
@@ -962,7 +992,7 @@
             pltpu.VMEM((2, nz) + each, F32),
             pltpu.VMEM((nz, per_dev // 2) + each, F32),
             one, one,
-            dma(n), dma(n),
+            dma(3 * n), dma(n),
             dma(2 * nz), dma(nz * per_dev),
             dma(nz), dma(nz),
             dma(3 * n), dma(k_all),
@@ -971,7 +1001,7 @@
             one, dma(4), one, dma(2),
             one, dma(2 * nz), one, dma(nz),
             dma(4), dma(2), one, dma(nz),
-            one, dma(n), one, dma(n),
+            one, one, one, one,
             dma(6), dma(6),
         ],
         compiler_params=pltpu.CompilerParams(

time: 59.6 us -> 58.3 us (0.978)
  Pallas kernels: 58.8 us -> 57.5 us
    pallas_call x1, Pallas kernels: 56.9 us -> 55.6 us  [per_device(): pl.pallas_call(functools.partial(kernel, n), out_shape=shape((n_ga, rows...]
where the time goes in v7:
time: 58.3 us; the launch traced here: 58.1 us
  Pallas kernels  57.5 us (99%)
  between operations  0.64 us (1%)
    pallas_call x1, Pallas kernels, per_device(): pl.pallas_call(functools.partial(kernel, n), out_shape=shape((n_ga, rows...  55.6 us
    pallas_call x1, Pallas kernels, per_device(): pl.pallas_call(layout, out_shape=[shape((rows, nt * nt), F32), shape((per...  1.91 us

profile of v7, /device:TPU:0, one launch (start us, length us, event | category | flops | bytes accessed | tf_op | source)
XLA Modules:
  0.0 58.1 jit_solution(4368579712299793825)
XLA Ops:
  0.6 55.6 %window.1.lines = f32[4,160,128]{2,1,0:T(8,128)} custom-call(s32[3,16]{1,0:T(4,128)} %bitcast.3, s32[16]{0:T(128)} %qs_ref.1, bf16[4,64,375]{2,1,0:T(8,128)(2,1)} %x_ref.1, bf16[4,64,375]{2,1,0:T(8,128)(2,1)} %y_ref.1, bf16[4,64,375]{2,1,0:T(8,128)(2,1)} %p_ref.1, f32[375]{0:T(512)} %v_ref.1, bf16[375,2,1500]{2,1,0:T(2,128)(2,1)} %bitcast.2), custom_call_target="tpu_custom_call" | custom-call | tf_op jit(solution)/shard_map/window/pallas_call | solution.py:955
  56.2 1.9 %layout.1 = (f32[16,4096]{1,0:T(8,128)}, f32[4,4096]{1,0:T(4,128)}) custom-call(f32[4,160,128]{2,1,0:T(8,128)} %window.1.lines), custom_call_target="tpu_custom_call" | custom-call | tf_op jit(solution)/shard_map/layout/pallas_call | solution.py:1012

commit v8 on v7

--- a/solution.py
+++ b/solution.py
@@ -69,6 +69,14 @@
         self.src, self.out, self.send, self.recv = src, out, send, recv
         self.size = src.shape[0]
         self.cut = cut
+
+    def landed(self, zz, same, k):
+        few = self.size - self.cut
+        if same:
+            return self.recv.at[zz * self.size + k]
+        if k >= self.cut:
+            return self.recv.at[self.nz * self.size + zz * few + k - self.cut]
+        return self.recv.at[self.nz * (self.size + few) + zz]
 
     def copy(self, zz, yy, k, way, own=False):
         at = (zz * 2 + yy) * self.size + k
@@ -80,23 +88,34 @@
         return remote(
             self.src.at[k] if own else block,
             block,
-            self.send.at[way * self.n + zz * 2 + yy],
-            self.recv.at[at],
+            self.send.at[way * self.nz + zz],
+            self.landed(zz, (yy is self.y) != (way == 2), k),
             {"ka": target},
         )
 
-    def all_sent(self, zz, yy, way, count):
-        block = self.out.at[pl.ds((zz * 2 + yy) * self.size, count)]
-        done = self.send.at[way * self.n + zz * 2 + yy]
+    def take(self, zz, yy, k):
+        block = self.out.at[(zz * 2 + yy) * self.size + k]
+        done = self.landed(zz, yy is self.y, k)
+        remote(block, block, done, done, {"ka": self.z * 2 + 1 - self.y}).wait_recv()
+
+    def some(self, count):
+        return self.out.at[pl.ds(0, count)]
+
+    def take_late(self, zz):
+        block, done = self.some(self.cut), self.landed(zz, False, 0)
+        remote(block, block, done, done, {"ka": self.z * 2 + 1 - self.y}).wait_recv()
+
+    def all_sent(self, zz, way, count):
+        block, done = self.some(count), self.send.at[way * self.nz + zz]
         remote(block, block, done, done, {"ka": self.z * 2 + 1 - self.y}).wait_send()
 
-    def chained(self, zz, yy, count, ways=(0, 1)):
+    def chained(self, zz, ways=(0, 1)):
         for way in ways:
             free = self.z < self.nz - 1 if way == 0 else self.z > 0
 
             @pl.when(free)
             def _(way=way):
-                self.all_sent(zz, yy, way, count)
+                self.all_sent(zz, way, 2 * self.size - self.cut)
 
     def chain(self, zz, yy, k, act, ways=(0, 1), own=False):
         for way in ways:
@@ -124,7 +143,7 @@
 
     def second(self):
         for k in self.early():
-            self.copy(self.z, 1 - self.y, k, 2).wait_recv()
+            self.take(self.z, 1 - self.y, k)
             self.chain(self.z, 1 - self.y, k, start)
 
     def sides(self, h, act):
@@ -138,7 +157,7 @@
 
     def hop(self, h, low=0, high=None):
         def one(k, yy, zz, way):
-            self.copy(zz, yy, k, 2).wait_recv()
+            self.take(zz, yy, k)
             self.chain(zz, yy, k, start, (way,))
 
         for k in range(self.size)[low:high]:
@@ -153,20 +172,15 @@
             self.sides(h, lambda zz, way, k=k: one(k, 1 - self.y, zz, way))
 
     def finish(self):
-        few = len(self.early())
-        self.chained(self.z, self.y, self.size)
-        self.all_sent(self.z, self.y, 2, self.size)
-        self.chained(self.z, 1 - self.y, few)
-        for k in range(self.cut):
-            self.copy(self.z, 1 - self.y, k, 2).wait_recv()
+        self.chained(self.z)
+        self.all_sent(self.z, 2, self.size)
+        self.take_late(self.z)
 
         def tail(h, carry):
             def side(zz, way):
-                self.chained(zz, self.y, self.size, (way,))
-                self.chained(zz, 1 - self.y, few, (way,))
-                self.all_sent(zz, self.y, 2, self.cut)
-                for k in range(self.cut):
-                    self.copy(zz, 1 - self.y, k, 2).wait_recv()
+                self.chained(zz, (way,))
+                self.all_sent(zz, 2, self.cut)
+                self.take_late(zz)
 
             self.sides(h, side)
             return carry
@@ -175,26 +189,21 @@
 
 
 class Rows(Gather):
-    def all_sent(self, zz, yy, way, count):
-        block = self.out.at[zz * 2 + yy]
-        done = self.send.at[way * self.n + zz * 2 + yy]
-        remote(block, block, done, done, {"ka": self.z * 2 + 1 - self.y}).wait_send()
+    def some(self, count):
+        return self.out.at[0]
 
     def begin(self):
         self.chain(self.z, self.y, 0, start, own=True)
         self.copy(self.z, self.y, 0, 2, True).start()
 
-    def other(self, zz):
-        self.copy(zz, 1 - self.y, 0, 2).wait_recv()
-
     def finish(self):
-        self.chained(self.z, self.y, 1)
-        self.all_sent(self.z, self.y, 2, 1)
+        self.chained(self.z)
+        self.all_sent(self.z, 2, 1)
 
         def tail(h, carry):
             def side(zz, way):
-                self.chained(zz, self.y, 1, (way,))
-                self.all_sent(zz, self.y, 2, 1)
+                self.chained(zz, (way,))
+                self.all_sent(zz, 2, 1)
 
             self.sides(h, side)
             return carry
@@ -220,28 +229,43 @@
             {"ka": target},
         )
 
-    def cross(self, zz, yy, i):
-        block = self.out.at[pl.ds((zz * 2 + yy) * self.size, self.size)]
+    def block(self, zz, yy):
+        return self.out.at[pl.ds((zz * 2 + yy) * self.size, self.size)]
+
+    def cross(self, i):
         return remote(
-            self.src if i == 0 and yy is self.y else block,
-            block,
+            self.src,
+            self.block(self.z, self.y),
             self.send.at[2 * self.nz + i],
             self.recv.at[self.nz * self.size + i],
             {"ka": self.z * 2 + 1 - self.y},
         )
 
-    def all_sent(self, zz, yy, way, count):
-        block = self.out.at[pl.ds((zz * 2 + yy) * self.size, count)]
-        done = self.send.at[way * self.nz + zz]
-        remote(block, block, done, done, {"ka": self.z * 2 + 1 - self.y}).wait_send()
-
-    def chained(self, zz, yy, count, ways=(0, 1)):
+    def crossed(self, zz, i):
+        block, done = self.block(zz, 1 - self.y), self.recv.at[self.nz * self.size + i]
+        remote(block, block, done, done, {"ka": self.z * 2 + 1 - self.y}).wait_recv()
+
+    def inward(self):
+        block = self.block(self.z, 1 - self.y)
+        return remote(
+            block,
+            block,
+            self.send.at[2 * self.nz + 2],
+            self.recv.at[self.nz * self.size + 1],
+            {"ka": jnp.where(self.z == 0, 1, self.nz - 2) * 2 + self.y},
+        )
+
+    def pass_inward(self):
+        self.crossed(self.z, 1)
+        self.inward().start()
+
+    def chained(self, zz, ways=(0, 1)):
         for way in ways:
             free = self.z <= self.nz - 3 if way == 0 else self.z >= 2
 
             @pl.when(free)
             def _(way=way):
-                self.all_sent(zz, yy, way, count)
+                self.all_sent(zz, way, self.size)
 
     def chain(self, zz, yy, k, act, ways=(0, 1), own=False):
         for way in ways:
@@ -256,9 +280,6 @@
             self.chain(self.z, self.y, k, start, own=True)
         self.out[pl.ds(self.me * self.size, self.size)] = self.src[...]
 
-    def across(self):
-        self.cross(self.z, self.y, 0).start()
-
     def hop(self, h):
         def own(zz, way):
             end = jnp.logical_and(self.edged, zz == self.edge)
@@ -272,18 +293,6 @@
 
         self.sides(h, own)
 
-    def crossed(self):
-        self.cross(self.z, 1 - self.y, 0).wait_recv()
-
-        @pl.when(self.edged)
-        def _():
-            self.cross(self.edge, 1 - self.y, 1).wait_recv()
-
-    def across_edge(self):
-        @pl.when(self.edged)
-        def _():
-            self.cross(self.edge, self.y, 1).start()
-
     def edge_in(self):
         @pl.when(self.edged)
         def _():
@@ -291,18 +300,19 @@
                 self.copy(self.edge, self.y, k, 2).wait_recv()
 
     def finish(self):
-        self.chained(self.z, self.y, self.size)
+        self.chained(self.z)
+
+        @pl.when(jnp.logical_not(self.inner))
+        def _():
+            self.cross(1).wait_send()
+            self.inward().wait_send()
 
         @pl.when(self.inner)
         def _():
-            self.cross(self.z, self.y, 0).wait_send()
-
-            @pl.when(self.edged)
-            def _():
-                self.cross(self.edge, self.y, 1).wait_send()
+            self.cross(0).wait_send()
 
             def tail(h, carry):
-                self.sides(h, lambda zz, way: self.chained(zz, self.y, self.size, (way,)))
+                self.sides(h, lambda zz, way: self.chained(zz, (way,)))
                 return carry
 
             lax.fori_loop(1, self.nz, tail, 0)
@@ -407,12 +417,13 @@
 
 
 class Reduce:
-    def __init__(self, part, out, recv1, tsend, recv2, s1, r1, s2, r2, per):
+    def __init__(self, part, out, recv1, tsend, recv2, s1, r1, s2, r2, per, lump):
         self.g = lax.axis_index("ga")
         self.x, self.c = self.g // 2, self.g % 2
         self.part, self.out = part, out
         self.recv1, self.tsend, self.recv2 = recv1, tsend, recv2
         self.s1, self.r1, self.s2, self.r2, self.per = s1, r1, s2, r2, per
+        self.lump, self.pieces = lump, part.shape[1] // per
 
     def rows(self, i):
         return pl.ds(i * self.per, self.per)
@@ -423,7 +434,7 @@
             self.part.at[xx * 2 + 1 - self.c, self.rows(i)],
             self.recv1.at[xx, self.rows(i)],
             self.s1,
-            self.r1.at[i * 2 + t],
+            self.r1.at[self.pieces + (0 if self.lump else i) if t else i],
             {"ga": self.x * 2 + 1 - self.c},
         )
 
@@ -432,7 +443,7 @@
             self.tsend.at[self.rows(i)],
             self.recv2.at[self.rows(i)],
             self.s2,
-            self.r2.at[i],
+            self.r2.at[0 if self.lump else i],
             {"ga": (1 - self.x) * 2 + self.c},
         )
 
@@ -449,10 +460,16 @@
         self.tsend[self.rows(i)] = self.sum_one(1 - self.x, i).astype(self.tsend.dtype)
         self.two(i).start()
 
+    def arrive(self):
+        to = {"ga": self.x * 2 + 1 - self.c}
+        for block, done in ((self.recv1.at[self.x], self.r1.at[self.pieces]), (self.recv2, self.r2.at[0])):
+            remote(block, block, done, done, to).wait_recv()
+
     def end(self, i):
-        self.one(1, i).wait_recv()
+        if not self.lump:
+            self.one(1, i).wait_recv()
+            self.two(i).wait_recv()
         v = self.sum_one(self.x, i)
-        self.two(i).wait_recv()
         v = (v + self.recv2[self.rows(i)].astype(F32)).astype(self.out.dtype)
         if len(self.out.shape) == len(self.tsend.shape):
             self.out[self.rows(i)] = v
@@ -529,12 +546,12 @@
     @pl.when(outer)
     def _():
         pg.first()
+        pg.cross(1).start()
         yg.first()
-        yg.across_late()
 
     @pl.when(pg.inner)
     def _():
-        pg.across()
+        pg.cross(0).start()
 
     fetch.wait()
     turn = 16
@@ -548,7 +565,7 @@
     lax.fori_loop(0, width // turn, relay, 0)
     if whole < width:
         w_ref[:, whole:] = jnp.swapaxes(wt[whole:], 0, 1)
-    red = Reduce(part, half, recv1, tsend, recv2, s1, r1, s2, r2, 2 * CAPQ)
+    red = Reduce(part, half, recv1, tsend, recv2, s1, r1, s2, r2, 2 * CAPQ, True)
 
     def multiply(v, a, r):
         w = tab[a, slots + me * CAPQ + r]
@@ -559,7 +576,7 @@
     def piece(zz):
         for r in range(CAPQ):
             multiply(xg.chosen(zz, me, r), zz * 2 + y, r)
-        rg.other(zz)
+        rg.take_late(zz)
         xg.across(zz).wait_recv()
         for r in range(CAPQ):
             multiply(x_got[zz * CAPQ + r], zz * 2 + 1 - y, r)
@@ -568,7 +585,7 @@
     quarter = nt // n_ga
     weight = v_ref[...].reshape(1, width)
     sets = jnp.where(pg.edged, 4, 2)
-    ered = Reduce(part3, eown, e1, et, e2, v1, w1, v2, w2, 4)
+    ered = Reduce(part3, eown, e1, et, e2, v1, w1, v2, w2, 4, True)
 
     def of(q):
         return jnp.where(q // 2 == 0, z, pg.edge) * 2 + q % 2
@@ -641,8 +658,12 @@
             @pl.when(pg.inner)
             def _():
                 pg.edge_in()
-                pg.across_edge()
-                yg.across_late()
+
+            @pl.when(outer)
+            def _():
+                pg.pass_inward()
+
+            yg.across_late()
 
             red.middle(z)
 
@@ -663,7 +684,12 @@
     @pl.when(pg.inner)
     def _():
         pg.hop(1)
-        pg.crossed()
+        pg.crossed(z, 0)
+
+        @pl.when(pg.edged)
+        def _():
+            pg.crossed(pg.edge, 1)
+
         lax.fori_loop(0, sets, weigh, 0)
         exchange(z)
 
@@ -703,6 +729,7 @@
         lax.fori_loop(2, nz, level, 0)
 
     xg.finish()
+    red.arrive()
     lax.fori_loop(0, nz, lambda i, c: (red.end(i), c)[1], 0)
     yg.finish()
     rg.finish()
@@ -718,9 +745,9 @@
         joined(both, part2, a)
         return carry
 
-    end = Reduce(part2, own, q1, qt, q2, t1, u1, t2, u2, n // 2)
-    for i in range(2):
-        lax.fori_loop(i * n // 2, (i + 1) * n // 2, source, 0, unroll=2)
+    end = Reduce(part2, own, q1, qt, q2, t1, u1, t2, u2, n // 4, False)
+    for i in range(4):
+        lax.fori_loop(i * n // 4, (i + 1) * n // 4, source, 0, unroll=2)
         end.begin(i)
     shape = own.shape[1:]
     left = lax.broadcasted_iota(I32, shape, 1) < nt
@@ -767,11 +794,12 @@
 
         lax.fori_loop(0, nz, one, 0)
 
-    end.middle(0)
-    end.middle(1)
+    for i in range(4):
+        end.middle(i)
 
     @pl.when(pg.inner)
     def _():
+        ered.arrive()
         lax.fori_loop(0, nz, lambda i, c: (ered.end(i), c)[1], 0)
         ered.finish()
         others(start)
@@ -799,17 +827,29 @@
         emir[z] = ebox[z]
 
     def cross(src, box, i, whose, ss, rs):
-        to = lax.rem(me + i, n)
-        return remote(src.at[to], box.at[whose], ss, rs, {"ka": to})
-
-    end.end(0)
-    end.end(1)
+        return remote(src.at[i], box.at[whose], ss, rs, {"ka": i})
+
+    def far_first(i):
+        return jnp.where(z < nz // 2, n - 1 - i, i)
+
+    for i in range(4):
+        end.end(i)
     end.finish()
-    lax.fori_loop(1, n, lambda i, c: (cross(own, inbox, i, me, as_, ar).start(), c)[1], 0)
+
+    def give(i, carry):
+        b = far_first(i)
+
+        @pl.when(b != me)
+        def _():
+            cross(own, inbox, b, me, as_, ar).start()
+
+        return carry
+
+    lax.fori_loop(0, n, give, 0)
     inbox[me] = own[me]
 
     def fill(i, carry):
-        b = lax.rem(me + i, n)
+        b = far_first(i)
 
         def add(a, sums):
             out = []
@@ -822,14 +862,13 @@
         for i_, v in enumerate(paired(sums)):
             outbox[b, i_] = v
 
-        @pl.when(i > 0)
-        def _():
-            cross(outbox, sumbox, i, me, bs, br).start()
+        @pl.when(b != me)
+        def _():
+            cross(outbox, sumbox, b, me, bs, br).start()
 
         return carry
 
-    lax.fori_loop(1, n, fill, 0)
-    fill(jnp.int32(0), 0)
+    lax.fori_loop(0, n, fill, 0)
     sumbox[me] = outbox[me]
     for yy in range(2):
 
@@ -874,7 +913,7 @@
 
     def spread(i, m, whose, to):
         block = lines.at[whose, parts[m]]
-        return remote(block, block, gs.at[i * 2 + m], gr.at[i * 2 + m], {"ga": to})
+        return remote(block, block, gs, gr.at[m if i == 0 else 2], {"ga": to})
 
     spread(0, 0, g, far).start()
     spread(1, 0, g, mate).start()
@@ -901,12 +940,12 @@
         rest = ebox.at[pl.ds(0, nz - 1)]
         remote(rest, rest, fs, fs, {"ka": z * 2 + 1 - y}).wait_send()
 
-    for m in range(2):
-        spread(1, m, mate, mate).wait_recv()
-        spread(2, m, (1 - x) * 2 + 1 - c, mate).wait_recv()
-        spread(0, m, g, far).wait_send()
-        spread(1, m, g, mate).wait_send()
-        spread(2, m, far, mate).wait_send()
+    for count, ss, rs in ((3, gs, None), (2, None, gr.at[2])):
+        block = lines.at[pl.ds(0, count)]
+        if rs is None:
+            remote(block, block, ss, ss, {"ga": mate}).wait_send()
+        else:
+            remote(block, block, rs, rs, {"ga": mate}).wait_recv()
 
 
 def layout(lines, blocks_ref, mirr_ref, turned, flat):
@@ -992,17 +1031,17 @@
             pltpu.VMEM((2, nz) + each, F32),
             pltpu.VMEM((nz, per_dev // 2) + each, F32),
             one, one,
-            dma(3 * n), dma(n),
+            dma(3 * nz), dma(2 * nz),
             dma(2 * nz), dma(nz * per_dev),
             dma(nz), dma(nz),
-            dma(3 * n), dma(k_all),
-            dma(2 * nz + 2), dma(nz * per_dev + 2),
-            one, dma(2 * nz), one, dma(nz),
-            one, dma(4), one, dma(2),
-            one, dma(2 * nz), one, dma(nz),
+            dma(3 * nz), dma(nz * (per_dev + 2)),
+            dma(2 * nz + 3), dma(nz * per_dev + 2),
+            one, dma(nz + 1), one, dma(1),
+            one, dma(8), one, dma(4),
+            one, dma(nz + 1), one, dma(1),
             dma(4), dma(2), one, dma(nz),
             one, one, one, one,
-            dma(6), dma(6),
+            one, dma(3),
         ],
         compiler_params=pltpu.CompilerParams(
             collective_id=0, has_side_effects=True, vmem_limit_bytes=LIMIT

time: 58.3 us -> 56.6 us (0.971)
  Pallas kernels: 57.5 us -> 55.7 us
    pallas_call x1, Pallas kernels: 55.6 us -> 53.8 us  [per_device(): pl.pallas_call(functools.partial(kernel, n), out_shape=shape((n_ga, rows...]
where the time goes in v8:
time: 56.6 us; the launch traced here: 56.4 us
  Pallas kernels  55.7 us (98%)
  between operations  0.64 us (1%)
    pallas_call x1, Pallas kernels, per_device(): pl.pallas_call(functools.partial(kernel, n), out_shape=shape((n_ga, rows...  53.8 us
    pallas_call x1, Pallas kernels, per_device(): pl.pallas_call(layout, out_shape=[shape((rows, nt * nt), F32), shape((per...  1.91 us

profile of v8, /device:TPU:0, one launch (start us, length us, event | category | flops | bytes accessed | tf_op | source)
XLA Modules:
  0.0 56.4 jit_solution(14914872866451952840)
XLA Ops:
  0.6 53.8 %window.1.lines = f32[4,160,128]{2,1,0:T(8,128)} custom-call(s32[3,16]{1,0:T(4,128)} %bitcast.3, s32[16]{0:T(128)} %qs_ref.1, bf16[4,64,375]{2,1,0:T(8,128)(2,1)} %x_ref.1, bf16[4,64,375]{2,1,0:T(8,128)(2,1)} %y_ref.1, bf16[4,64,375]{2,1,0:T(8,128)(2,1)} %p_ref.1, f32[375]{0:T(512)} %v_ref.1, bf16[375,2,1500]{2,1,0:T(2,128)(2,1)} %bitcast.2), custom_call_target="tpu_custom_call" | custom-call | tf_op jit(solution)/shard_map/window/pallas_call | solution.py:994
  54.5 1.9 %layout.1 = (f32[16,4096]{1,0:T(8,128)}, f32[4,4096]{1,0:T(4,128)}) custom-call(f32[4,160,128]{2,1,0:T(8,128)} %window.1.lines), custom_call_target="tpu_custom_call" | custom-call | tf_op jit(solution)/shard_map/layout/pallas_call | solution.py:1051

commit v9 on v8

--- a/solution.py
+++ b/solution.py
@@ -135,7 +135,6 @@
     def across_late(self):
         for k in range(self.cut):
             self.copy(self.z, self.y, k, 2, True).start()
-        self.out[pl.ds(self.me * self.size, self.size)] = self.src[...]
 
     def first(self):
         for k in range(self.size):
@@ -278,7 +277,6 @@
     def first(self):
         for k in range(self.size):
             self.chain(self.z, self.y, k, start, own=True)
-        self.out[pl.ds(self.me * self.size, self.size)] = self.src[...]
 
     def hop(self, h):
         def own(zz, way):
@@ -358,7 +356,6 @@
     def first(self):
         for k in range(self.size):
             self.chain(self.z, k, start, own=True)
-        self.col[pl.ds(self.z * self.size, self.size)] = self.src[...]
 
     def hop(self, h):
         for k in range(self.size):
@@ -514,7 +511,7 @@
            tab, at_ref, row_ref, wt, w_ref, x_col, x_out, x_got, y_all, p_all, part, half,
            recv1, tsend, recv2, part2, own, q1, qt, q2, second, outbox, sumbox, inbox,
            split, part3, eown, e1, et, e2, ebox, ein, emir,
-           ws, ls, ts, tr, xs, xr, xps, xpr, ys, yr, ps, pr, s1, r1, s2, r2, t1, u1, t2, u2,
+           ws, ls, ks, ts, tr, xs, xr, xps, xpr, ys, yr, ps, pr, s1, r1, s2, r2, t1, u1, t2, u2,
            v1, w1, v2, w2, es, er, fs, fr, as_, ar, bs, br, gs, gr):
     per_dev, nt, width = x_ref.shape
     rows = pairs_ref.shape[1]
@@ -527,6 +524,14 @@
     z, y = me // 2, me % 2
     fetch = pltpu.make_async_copy(w_hbm, wt, ws)
     fetch.start()
+    mine = pl.ds(me * per_dev, per_dev)
+    keeps = [
+        pltpu.make_async_copy(x_ref, x_col.at[pl.ds(z * per_dev, per_dev)], ks.at[0]),
+        pltpu.make_async_copy(p_ref, p_all.at[mine], ks.at[1]),
+        pltpu.make_async_copy(y_ref, y_all.at[mine], ks.at[2]),
+    ]
+    for c in keeps:
+        c.start()
     greet(n, lambda: make_row(n, q_slots, per_dev, pairs_ref, qs_ref, row_ref, at_ref))
     xg = Pick(n, x_ref, x_col, x_out, x_got, tab, xs, xr, xps, xpr)
     yg = Gather(n, y_ref, y_all, ys, yr, per_dev - 1)
@@ -539,6 +544,8 @@
     xg.first()
     keep.start()
     keep.wait()
+    for c in keeps:
+        c.wait()
     xg.pass_on(z)
 
     yg.across_early()
@@ -585,7 +592,7 @@
     quarter = nt // n_ga
     weight = v_ref[...].reshape(1, width)
     sets = jnp.where(pg.edged, 4, 2)
-    ered = Reduce(part3, eown, e1, et, e2, v1, w1, v2, w2, 4, True)
+    ered = Reduce(part3, eown, e1, et, e2, v1, w1, v2, w2, 4, False)
 
     def of(q):
         return jnp.where(q // 2 == 0, z, pg.edge) * 2 + q % 2
@@ -625,6 +632,54 @@
         lax.fori_loop(0, sets, one, 0)
         ered.begin(zz)
 
+    shape = own.shape[1:]
+    left = lax.broadcasted_iota(I32, shape, 1) < nt
+    doubles = per_dev // 2
+
+    def paired(sums):
+        sums = [v[:, :nt] + v[:, nt:] for v in sums]
+        return [
+            jnp.concatenate([sums[i], sums[i + doubles]], axis=1) for i in range(doubles)
+        ]
+
+    def to_first(q, zz):
+        return remote(eown.at[zz, q], ein.at[y, zz], es, er.at[y], {"ka": of(q)})
+
+    def to_second(zz):
+        return remote(ebox.at[zz], emir.at[z], fs, fr.at[z], {"ka": zz * 2 + y})
+
+    def deliver(zz):
+        ered.end(zz)
+
+        def give(q, carry):
+            @pl.when(q != y)
+            def _():
+                to_first(q, zz).start()
+
+            return carry
+
+        lax.fori_loop(0, sets, give, 0)
+        ein[y, zz] = eown[zz, y]
+
+        def add(q, sums):
+            at = 4 * slots + (zz * 2 + y) * CAPQ
+            k2 = jnp.where(left, tab[of(q), at], tab[of(q), at + 1])
+            v = eown[zz, q]
+            base = (zz * 2 + y) * per_dev
+            return tuple(t + jnp.where(k2 == base + i, v, 0.0) for i, t in enumerate(sums))
+
+        sums = lax.fori_loop(0, sets, add, tuple(jnp.zeros(shape, F32) for _ in range(per_dev)))
+        for i, v in enumerate(paired(sums)):
+            ebox[zz, i] = v
+
+        @pl.when(zz != z)
+        def _():
+            to_second(zz).start()
+
+        @pl.when(zz == z)
+        def _():
+            emir[z] = ebox[z]
+
     rg.hop(1)
     xg.hop(1)
 
@@ -720,20 +775,9 @@
     pg.finish()
     yg.hop(nz - 1)
 
-    @pl.when(pg.inner)
-    def _():
-        def level(h, carry):
-            pg.sides(h, lambda zz, way: ered.middle(zz))
-            return carry
-
-        lax.fori_loop(2, nz, level, 0)
-
-    xg.finish()
     red.arrive()
     lax.fori_loop(0, nz, lambda i, c: (red.end(i), c)[1], 0)
     yg.finish()
-    rg.finish()
-    red.finish()
 
     def source(a, carry):
         both = []
@@ -749,16 +793,6 @@
     for i in range(4):
         lax.fori_loop(i * n // 4, (i + 1) * n // 4, source, 0, unroll=2)
         end.begin(i)
-    shape = own.shape[1:]
-    left = lax.broadcasted_iota(I32, shape, 1) < nt
-    doubles = per_dev // 2
-
-    def paired(sums):
-        sums = [v[:, :nt] + v[:, nt:] for v in sums]
-        return [
-            jnp.concatenate([sums[i], sums[i + doubles]], axis=1) for i in range(doubles)
-        ]
-
     def seconds(a, carry):
         at = 2 * slots + me * CAPQ
         second[a] = jnp.where(left, tab[a, at], tab[a, at + 1])
@@ -766,65 +800,27 @@
 
     lax.fori_loop(0, n, seconds, 0)
 
-    def to_first(q):
-        return remote(
-            eown.at[:, q], ein.at[y], es.at[q], er.at[y], {"ka": of(q)}
-        )
-
-    def to_second(zz):
-        return remote(ebox.at[zz], emir.at[z], fs, fr.at[z], {"ka": zz * 2 + y})
-
-    def others(act):
-        def one(q, carry):
-            @pl.when(q != y)
-            def _():
-                act(to_first(q))
-
+    @pl.when(pg.inner)
+    def _():
+        def level(h, carry):
+            pg.sides(h, lambda zz, way: ered.middle(zz))
             return carry
 
-        lax.fori_loop(0, sets, one, 0)
-
-    def levels(act):
-        def one(zz, carry):
-            @pl.when(zz != z)
-            def _():
-                act(to_second(zz))
-
-            return carry
-
-        lax.fori_loop(0, nz, one, 0)
+        lax.fori_loop(2, nz, level, 0)
 
     for i in range(4):
         end.middle(i)
 
     @pl.when(pg.inner)
     def _():
-        ered.arrive()
-        lax.fori_loop(0, nz, lambda i, c: (ered.end(i), c)[1], 0)
-        ered.finish()
-        others(start)
-        ein[y] = eown[:, y]
-
-        def level(zz, carry):
-            def add(q, sums):
-                at = 4 * slots + (zz * 2 + y) * CAPQ
-                k2 = jnp.where(left, tab[of(q), at], tab[of(q), at + 1])
-                v = eown[zz, q]
-                base = (zz * 2 + y) * per_dev
-                return tuple(
-                    t + jnp.where(k2 == base + i, v, 0.0) for i, t in enumerate(sums)
-                )
-
-            sums = lax.fori_loop(
-                0, sets, add, tuple(jnp.zeros(shape, F32) for _ in range(per_dev))
-            )
-            for i, v in enumerate(paired(sums)):
-                ebox[zz, i] = v
+        deliver(z)
+
+        def level(h, carry):
+            pg.sides(h, lambda zz, way: deliver(zz))
             return carry
 
-        lax.fori_loop(0, nz, level, 0)
-        levels(start)
-        emir[z] = ebox[z]
+        lax.fori_loop(1, nz, level, 0)
+
 
     def cross(src, box, i, whose, ss, rs):
         return remote(src.at[i], box.at[whose], ss, rs, {"ka": i})
@@ -834,7 +830,6 @@
 
     for i in range(4):
         end.end(i)
-    end.finish()
 
     def give(i, carry):
         b = far_first(i)
@@ -847,6 +842,7 @@
 
     lax.fori_loop(0, n, give, 0)
     inbox[me] = own[me]
+
 
     def fill(i, carry):
         b = far_first(i)
@@ -874,7 +870,7 @@
 
         @pl.when(jnp.logical_or(jnp.logical_not(pg.inner), yy != y))
         def _(yy=yy):
-            remote(ein.at[yy], ein.at[yy], es.at[0], er.at[yy], {"ka": z * 2 + 1 - y}).wait_recv()
+            remote(ein.at[yy], ein.at[yy], es, er.at[yy], {"ka": z * 2 + 1 - y}).wait_recv()
 
     def inner_level(zz, carry):
         @pl.when(zz != z)
@@ -917,6 +913,10 @@
 
     spread(0, 0, g, far).start()
     spread(1, 0, g, mate).start()
+    xg.finish()
+    rg.finish()
+    red.finish()
+    end.finish()
     arrived(sumbox, br)
     for i in range(doubles):
         total = lax.fori_loop(
@@ -936,7 +936,14 @@
         remote(rest, rest, ss, ss, {"ka": z * 2 + 1 - y}).wait_send()
     @pl.when(pg.inner)
     def _():
-        others(sent)
+        ered.finish()
+        for edged, count in ((True, 3), (False, 1)):
+
+            @pl.when(pg.edged if edged else jnp.logical_not(pg.edged))
+            def _(count=count):
+                sent_lines = eown.at[:, pl.ds(0, count)]
+                remote(sent_lines, sent_lines, es, es, {"ka": z * 2 + 1 - y}).wait_send()
+
         rest = ebox.at[pl.ds(0, nz - 1)]
         remote(rest, rest, fs, fs, {"ka": z * 2 + 1 - y}).wait_send()
 
@@ -994,7 +1001,7 @@
     lines = pl.pallas_call(
         functools.partial(kernel, n),
         out_shape=shape((n_ga, rows * quarter // 2 + per_dev // 2 * quarter, CAPQ * nt), F32),
-        in_specs=[SM, SM, VM, VM, VM, VM, HB],
+        in_specs=[SM, SM, HB, HB, HB, VM, HB],
         out_specs=VM,
         scratch_shapes=[
             pltpu.SMEM((n, row_len), I32),
@@ -1030,7 +1037,7 @@
             pltpu.VMEM((nz, per_dev // 2) + each, F32),
             pltpu.VMEM((2, nz) + each, F32),
             pltpu.VMEM((nz, per_dev // 2) + each, F32),
-            one, one,
+            one, one, dma(3),
             dma(3 * nz), dma(2 * nz),
             dma(2 * nz), dma(nz * per_dev),
             dma(nz), dma(nz),
@@ -1038,8 +1045,8 @@
             dma(2 * nz + 3), dma(nz * per_dev + 2),
             one, dma(nz + 1), one, dma(1),
             one, dma(8), one, dma(4),
-            one, dma(nz + 1), one, dma(1),
-            dma(4), dma(2), one, dma(nz),
+            one, dma(2 * nz), one, dma(nz),
+            one, dma(2), one, dma(nz),
             one, one, one, one,
             one, dma(3),
         ],

time: 56.6 us -> 56.3 us (level)
  no operation moved by 1% of the time
where the time goes in v9:
time: 56.3 us; the launch traced here: 56.1 us
  Pallas kernels  55.4 us (98%)
  between operations  0.64 us (1%)
    pallas_call x1, Pallas kernels, per_device(): pl.pallas_call(functools.partial(kernel, n), out_shape=shape((n_ga, rows...  53.5 us
    pallas_call x1, Pallas kernels, per_device(): pl.pallas_call(layout, out_shape=[shape((rows, nt * nt), F32), shape((per...  1.91 us

profile of v9, /device:TPU:0, one launch (start us, length us, event | category | flops | bytes accessed | tf_op | source)
XLA Modules:
  0.0 56.1 jit_solution(10095784360301324620)
XLA Ops:
  0.6 53.5 %window.1.lines = f32[4,160,128]{2,1,0:T(8,128)} custom-call(s32[3,16]{1,0:T(4,128)} %bitcast.3, s32[16]{0:T(128)} %qs_ref.1, bf16[4,64,375]{2,1,0:T(8,128)(2,1)} %x_ref.1, bf16[4,64,375]{2,1,0:T(8,128)(2,1)} %y_ref.1, bf16[4,64,375]{2,1,0:T(8,128)(2,1)} %p_ref.1, f32[375]{0:T(512)} %v_ref.1, bf16[375,2,1500]{2,1,0:T(2,128)(2,1)} %bitcast.2), custom_call_target="tpu_custom_call" | custom-call | tf_op jit(solution)/shard_map/window/pallas_call | solution.py:1001
  54.2 1.9 %layout.1 = (f32[16,4096]{1,0:T(8,128)}, f32[4,4096]{1,0:T(4,128)}) custom-call(f32[4,160,128]{2,1,0:T(8,128)} %window.1.lines), custom_call_target="tpu_custom_call" | custom-call | tf_op jit(solution)/shard_map/layout/pallas_call | solution.py:1058

commit v10 on v9

--- a/solution.py
+++ b/solution.py
@@ -507,8 +507,8 @@
     row_ref[...] = row
 
 
-def kernel(n, pairs_ref, qs_ref, x_ref, y_ref, p_ref, v_ref, w_hbm, lines,
-           tab, at_ref, row_ref, wt, w_ref, x_col, x_out, x_got, y_all, p_all, part, half,
+def kernel(n, pairs_hbm, qs_hbm, x_ref, y_ref, p_ref, v_hbm, w_hbm, lines,
+           pairs_ref, qs_ref, v_ref, tab, at_ref, row_ref, wt, w_ref, x_col, x_out, x_got, y_all, p_all, part, half,
            recv1, tsend, recv2, part2, own, q1, qt, q2, second, outbox, sumbox, inbox,
            split, part3, eown, e1, et, e2, ebox, ein, emir,
            ws, ls, ks, ts, tr, xs, xr, xps, xpr, ys, yr, ps, pr, s1, r1, s2, r2, t1, u1, t2, u2,
@@ -523,6 +523,14 @@
     g = lax.axis_index("ga")
     z, y = me // 2, me % 2
     fetch = pltpu.make_async_copy(w_hbm, wt, ws)
+    lists = [
+        pltpu.make_async_copy(pairs_hbm, pairs_ref, ks.at[3]),
+        pltpu.make_async_copy(qs_hbm, qs_ref, ks.at[4]),
+    ]
+    for c in lists:
+        c.start()
+    weights = pltpu.make_async_copy(v_hbm, v_ref, ks.at[5])
+    weights.start()
     fetch.start()
     mine = pl.ds(me * per_dev, per_dev)
     keeps = [
@@ -532,7 +540,13 @@
     ]
     for c in keeps:
         c.start()
-    greet(n, lambda: make_row(n, q_slots, per_dev, pairs_ref, qs_ref, row_ref, at_ref))
+
+    def table():
+        for c in lists:
+            c.wait()
+        make_row(n, q_slots, per_dev, pairs_ref, qs_ref, row_ref, at_ref)
+
+    greet(n, table)
     xg = Pick(n, x_ref, x_col, x_out, x_got, tab, xs, xr, xps, xpr)
     yg = Gather(n, y_ref, y_all, ys, yr, per_dev - 1)
     pg = Hub(n, p_ref, p_all, ps, pr)
@@ -590,6 +604,7 @@
         red.begin(zz)
 
     quarter = nt // n_ga
+    weights.wait()
     weight = v_ref[...].reshape(1, width)
     sets = jnp.where(pg.edged, 4, 2)
     ered = Reduce(part3, eown, e1, et, e2, v1, w1, v2, w2, 4, False)
@@ -926,11 +941,13 @@
             2, nz - 1, lambda zz, t, i=i: t + emir[zz, i], emir[1, i]
         )
         lines[g, pl.ds(base + i * quarter, quarter)] = 2.0 * term - total
+    diag = (1 - x) * 2 + 1 - c
     spread(0, 1, g, far).start()
+    spread(2, 1, g, diag).start()
     spread(1, 1, g, mate).start()
-    for m in range(2):
-        spread(0, m, far, far).wait_recv()
-        spread(2, m, far, mate).start()
+    spread(0, 0, far, far).wait_recv()
+    spread(2, 0, far, mate).start()
+    spread(0, 1, far, far).wait_recv()
     for src, ss in ((own, as_), (outbox, bs)):
         rest = src.at[pl.ds(0, n - 1)]
         remote(rest, rest, ss, ss, {"ka": z * 2 + 1 - y}).wait_send()
@@ -1001,9 +1018,12 @@
     lines = pl.pallas_call(
         functools.partial(kernel, n),
         out_shape=shape((n_ga, rows * quarter // 2 + per_dev // 2 * quarter, CAPQ * nt), F32),
-        in_specs=[SM, SM, HB, HB, HB, VM, HB],
+        in_specs=[HB] * 7,
         out_specs=VM,
         scratch_shapes=[
+            pltpu.SMEM((pairs.shape[1], rows), I32),
+            pltpu.SMEM(q_slot.shape, I32),
+            pltpu.VMEM((g,), F32),
             pltpu.SMEM((n, row_len), I32),
             pltpu.SMEM((2, rows), I32),
             pltpu.VMEM((1, row_len), I32),
@@ -1037,7 +1057,7 @@
             pltpu.VMEM((nz, per_dev // 2) + each, F32),
             pltpu.VMEM((2, nz) + each, F32),
             pltpu.VMEM((nz, per_dev // 2) + each, F32),
-            one, one, dma(3),
+            one, one, dma(6),
             dma(3 * nz), dma(2 * nz),
             dma(2 * nz), dma(nz * per_dev),
             dma(nz), dma(nz),

time: 56.3 us -> 55.1 us (0.979)
  Pallas kernels: 55.4 us -> 54.3 us
    pallas_call x1, Pallas kernels: 53.5 us -> 52.4 us  [per_device(): pl.pallas_call(functools.partial(kernel, n), out_shape=shape((n_ga, rows...]
where the time goes in v10:
time: 55.1 us; the launch traced here: 55 us
  Pallas kernels  54.3 us (99%)
  between operations  0.64 us (1%)
    pallas_call x1, Pallas kernels, per_device(): pl.pallas_call(functools.partial(kernel, n), out_shape=shape((n_ga, rows...  52.4 us
    pallas_call x1, Pallas kernels, per_device(): pl.pallas_call(layout, out_shape=[shape((rows, nt * nt), F32), shape((per...  1.91 us

profile of v10, /device:TPU:0, one launch (start us, length us, event | category | flops | bytes accessed | tf_op | source)
XLA Modules:
  0.0 55.0 jit_solution(12267883785184346160)
XLA Ops:
  0.6 52.4 %window.1.lines = f32[4,160,128]{2,1,0:T(8,128)} custom-call(s32[3,16]{1,0:T(4,128)} %bitcast.3, s32[16]{0:T(128)} %qs_hbm.1, bf16[4,64,375]{2,1,0:T(8,128)(2,1)} %x_ref.1, bf16[4,64,375]{2,1,0:T(8,128)(2,1)} %y_ref.1, bf16[4,64,375]{2,1,0:T(8,128)(2,1)} %p_ref.1, f32[375]{0:T(512)} %v_hbm.1, bf16[375,2,1500]{2,1,0:T(2,128)(2,1)} %bitcast.2), custom_call_target="tpu_custom_call" | custom-call | tf_op jit(solution)/shard_map/window/pallas_call | solution.py:1018
  53.1 1.9 %layout.1 = (f32[16,4096]{1,0:T(8,128)}, f32[4,4096]{1,0:T(4,128)}) custom-call(f32[4,160,128]{2,1,0:T(8,128)} %window.1.lines), custom_call_target="tpu_custom_call" | custom-call | tf_op jit(solution)/shard_map/layout/pallas_call | solution.py:1078

commit v11 on v10

--- a/solution.py
+++ b/solution.py
@@ -920,14 +920,18 @@
     base = rows * sub
     x, c = g // 2, g % 2
     mate, far = x * 2 + 1 - c, (1 - x) * 2 + c
-    parts = (pl.ds(0, base), pl.ds(base, doubles * quarter))
+    parts = (pl.ds(0, base // 2), pl.ds(base, doubles * quarter), pl.ds(base // 2, base // 2))
 
     def spread(i, m, whose, to):
         block = lines.at[whose, parts[m]]
-        return remote(block, block, gs, gr.at[m if i == 0 else 2], {"ga": to})
-
+        return remote(block, block, gs, gr.at[m if i == 0 else 3], {"ga": to})
+
+    diag = (1 - x) * 2 + 1 - c
     spread(0, 0, g, far).start()
+    spread(0, 2, g, far).start()
+    spread(2, 2, g, diag).start()
     spread(1, 0, g, mate).start()
+    spread(1, 2, g, mate).start()
     xg.finish()
     rg.finish()
     red.finish()
@@ -941,12 +945,12 @@
             2, nz - 1, lambda zz, t, i=i: t + emir[zz, i], emir[1, i]
         )
         lines[g, pl.ds(base + i * quarter, quarter)] = 2.0 * term - total
-    diag = (1 - x) * 2 + 1 - c
     spread(0, 1, g, far).start()
     spread(2, 1, g, diag).start()
     spread(1, 1, g, mate).start()
     spread(0, 0, far, far).wait_recv()
     spread(2, 0, far, mate).start()
+    spread(0, 2, far, far).wait_recv()
     spread(0, 1, far, far).wait_recv()
     for src, ss in ((own, as_), (outbox, bs)):
         rest = src.at[pl.ds(0, n - 1)]
@@ -964,7 +968,7 @@
         rest = ebox.at[pl.ds(0, nz - 1)]
         remote(rest, rest, fs, fs, {"ka": z * 2 + 1 - y}).wait_send()
 
-    for count, ss, rs in ((3, gs, None), (2, None, gr.at[2])):
+    for count, ss, rs in ((3, gs, None), (2, None, gr.at[3])):
         block = lines.at[pl.ds(0, count)]
         if rs is None:
             remote(block, block, ss, ss, {"ga": mate}).wait_send()
@@ -1068,7 +1072,7 @@
             one, dma(2 * nz), one, dma(nz),
             one, dma(2), one, dma(nz),
             one, one, one, one,
-            one, dma(3),
+            one, dma(4),
         ],
         compiler_params=pltpu.CompilerParams(
             collective_id=0, has_side_effects=True, vmem_limit_bytes=LIMIT

time: 55.1 us -> 54.8 us (level)
  no operation moved by 1% of the time
where the time goes in v11:
time: 54.8 us; the launch traced here: 54.6 us
  Pallas kernels  54 us (99%)
  between operations  0.64 us (1%)
    pallas_call x1, Pallas kernels, per_device(): pl.pallas_call(functools.partial(kernel, n), out_shape=shape((n_ga, rows...  52.1 us
    pallas_call x1, Pallas kernels, per_device(): pl.pallas_call(layout, out_shape=[shape((rows, nt * nt), F32), shape((per...  1.91 us

profile of v11, /device:TPU:0, one launch (start us, length us, event | category | flops | bytes accessed | tf_op | source)
XLA Modules:
  0.0 54.6 jit_solution(4813937462917328523)
XLA Ops:
  0.6 52.1 %window.1.lines = f32[4,160,128]{2,1,0:T(8,128)} custom-call(s32[3,16]{1,0:T(4,128)} %bitcast.3, s32[16]{0:T(128)} %qs_hbm.1, bf16[4,64,375]{2,1,0:T(8,128)(2,1)} %x_ref.1, bf16[4,64,375]{2,1,0:T(8,128)(2,1)} %y_ref.1, bf16[4,64,375]{2,1,0:T(8,128)(2,1)} %p_ref.1, f32[375]{0:T(512)} %v_hbm.1, bf16[375,2,1500]{2,1,0:T(2,128)(2,1)} %bitcast.2), custom_call_target="tpu_custom_call" | custom-call | tf_op jit(solution)/shard_map/window/pallas_call | solution.py:1022
  52.7 1.9 %layout.1 = (f32[16,4096]{1,0:T(8,128)}, f32[4,4096]{1,0:T(4,128)}) custom-call(f32[4,160,128]{2,1,0:T(8,128)} %window.1.lines), custom_call_target="tpu_custom_call" | custom-call | tf_op jit(solution)/shard_map/layout/pallas_call | solution.py:1082

commit v12 on v11

--- a/solution.py
+++ b/solution.py
@@ -541,22 +541,23 @@
     for c in keeps:
         c.start()
 
+    keep = pltpu.make_async_copy(row_ref.at[0], tab.at[me], ls)
+
     def table():
         for c in lists:
             c.wait()
         make_row(n, q_slots, per_dev, pairs_ref, qs_ref, row_ref, at_ref)
+        keep.start()
 
     greet(n, table)
     xg = Pick(n, x_ref, x_col, x_out, x_got, tab, xs, xr, xps, xpr)
     yg = Gather(n, y_ref, y_all, ys, yr, per_dev - 1)
     pg = Hub(n, p_ref, p_all, ps, pr)
     outer = jnp.logical_not(pg.inner)
-    keep = pltpu.make_async_copy(row_ref.at[0], tab.at[me], ls)
 
     rg = Rows(n, row_ref, tab, ts, tr, 1)
     rg.begin()
     xg.first()
-    keep.start()
     keep.wait()
     for c in keeps:
         c.wait()

time: 54.8 us -> 54.4 us (level)
  no operation moved by 1% of the time
where the time goes in v12:
time: 54.4 us; the launch traced here: 54.2 us
  Pallas kernels  53.6 us (99%)
  between operations  0.64 us (1%)
    pallas_call x1, Pallas kernels, per_device(): pl.pallas_call(functools.partial(kernel, n), out_shape=shape((n_ga, rows...  51.7 us
    pallas_call x1, Pallas kernels, per_device(): pl.pallas_call(layout, out_shape=[shape((rows, nt * nt), F32), shape((per...  1.91 us

profile of v12, /device:TPU:0, one launch (start us, length us, event | category | flops | bytes accessed | tf_op | source)
XLA Modules:
  0.0 54.2 jit_solution(11235486038411647074)
XLA Ops:
  0.6 51.7 %window.1.lines = f32[4,160,128]{2,1,0:T(8,128)} custom-call(s32[3,16]{1,0:T(4,128)} %bitcast.3, s32[16]{0:T(128)} %qs_hbm.1, bf16[4,64,375]{2,1,0:T(8,128)(2,1)} %x_ref.1, bf16[4,64,375]{2,1,0:T(8,128)(2,1)} %y_ref.1, bf16[4,64,375]{2,1,0:T(8,128)(2,1)} %p_ref.1, f32[375]{0:T(512)} %v_hbm.1, bf16[375,2,1500]{2,1,0:T(2,128)(2,1)} %bitcast.2), custom_call_target="tpu_custom_call" | custom-call | tf_op jit(solution)/shard_map/window/pallas_call | solution.py:1023
  52.3 1.9 %layout.1 = (f32[16,4096]{1,0:T(8,128)}, f32[4,4096]{1,0:T(4,128)}) custom-call(f32[4,160,128]{2,1,0:T(8,128)} %window.1.lines), custom_call_target="tpu_custom_call" | custom-call | tf_op jit(solution)/shard_map/layout/pallas_call | solution.py:1083
